TPU v7x, 512 devices: a whole 4x8x8 slice. The times are simulated.
512 devices in a mesh: sensor: 128 (over y_lo, z, x, core), batch: 4 (over y_hi).
Axes of the slice: x: 4, y: 8 (y_hi: 4, y_lo: 2; y = y_hi * 2 + y_lo), z: 8, core: 2. Of those that a mesh axis runs over, the one named last changes fastest.
Arguments:
- samples: bfloat16 [512, 262144], P('batch', 'sensor'), may hold values from -24 to 24
- branch_weight: bfloat16 [262144, 2048], P('sensor', 'batch'), may hold values from -0.01171875 to 0.01171875
- branch_bias: float32 [2048], P('batch'), may hold values from -3 to 3
- upstream: bfloat16 [512, 2048], P('sensor', 'batch'), may hold values from -0.29882812 to 0.29882812
Outputs:
- activation: bfloat16 [512, 2048], P('sensor', 'batch')
- weight_grad: bfloat16 [262144, 2048], P('sensor', 'batch')
- bias_grad: float32 [2048], P('batch')
All inputs are finite; a program needn't handle non-finite values.
Results may differ from a plain program's by a relative error of at most 0.005.
Values may be sent and summed in bfloat16 or wider, within the bound.
A program may use at most 64 MiB of HBM per device.

v0:
```python
import jax
import jax.numpy as jnp
from jax import lax
from jax.sharding import Mesh
from jax.sharding import PartitionSpec as P

SENSOR = ("sensor_0", "sensor_1", "sensor_2", "sensor_3")


def copy_for_each(array, axis):
    copies = jnp.broadcast_to(array, (lax.axis_size(axis), *array.shape))
    return lax.all_to_all(copies, axis, split_axis=0, concat_axis=0, tiled=True)


def joined_along(pieces, dim):
    pieces = jnp.moveaxis(pieces, 0, dim)
    lengths = pieces.shape
    return pieces.reshape(*lengths[:dim], lengths[dim] * lengths[dim + 1], *lengths[dim + 2 :])


def collect(array, axis, dim):
    pieces = copy_for_each(array, axis)
    return joined_along(pieces, dim)


def in_blocks(array, dim, size):
    lengths = array.shape
    pieces = array.reshape(*lengths[:dim], size, lengths[dim] // size, *lengths[dim + 1 :])
    return jnp.moveaxis(pieces, dim, 0)


def sum_at_owner(array, axis, dim):
    pieces = in_blocks(array, dim, lax.axis_size(axis))
    arrived = lax.all_to_all(pieces, axis, split_axis=0, concat_axis=0, tiled=True)
    return arrived.sum(axis=0)


def summed_rows(array, axes, dim):
    far, near = axes
    pieces = in_blocks(array, dim, lax.axis_size(far))
    nearer = sum_at_owner(pieces, near, dim + 1)
    arrived = lax.all_to_all(nearer, far, split_axis=0, concat_axis=0, tiled=True)
    return arrived.sum(axis=0)


def gather_axes(array, axes, dim):
    far, near = axes
    leading = copy_for_each(array, far)
    pieces = jnp.swapaxes(copy_for_each(leading, near), 0, 1)
    return joined_along(pieces.reshape(-1, *array.shape), dim)


def body(samples, branch_weight, branch_bias, upstream):
    all_rows = collect(samples, "batch", 0)
    partial_value = jnp.dot(all_rows, branch_weight, preferred_element_type=jnp.float32)
    summed = summed_rows(partial_value, (("sensor_0", "sensor_1", "sensor_2"), "sensor_3"), 0)
    pre = summed + branch_bias[None, :]
    act_full = jnp.tanh(pre)
    activation = act_full.astype(jnp.bfloat16)
    grad_pre = (upstream.astype(jnp.float32) * (1.0 - act_full * act_full)).astype(jnp.bfloat16)
    grad_all = gather_axes(grad_pre, (("sensor_0", "sensor_1", "sensor_2"), "sensor_3"), 0)
    weight_full = lax.dot_general(
        all_rows, grad_all, (((0,), (0,)), ((), ())), preferred_element_type=jnp.float32
    )
    row_total = jnp.sum(grad_all.astype(jnp.float32), axis=0)
    weight_grad = weight_full.astype(jnp.bfloat16)
    return (activation, weight_grad, row_total)


def solution(mesh):
    torus = Mesh(
        mesh.devices.reshape(2, 8, 4, 2, mesh.shape["batch"]),
        ("sensor_0", "sensor_1", "sensor_2", "sensor_3", "batch"),
    )
    in_specs = (P("batch", SENSOR), P(SENSOR, "batch"), P("batch"), P(SENSOR, "batch"))
    out_specs = (P(SENSOR, "batch"), P(SENSOR, "batch"), P("batch"))
    return jax.shard_map(body, mesh=torus, in_specs=in_specs, out_specs=out_specs, check_vma=False)
```

profile of v0, /device:TPU:1, one launch (start us, length us, event | category | flops | bytes accessed | tf_op | source)
XLA Modules:
  0.0 139.1 jit_solution(1608312200760354640)
XLA Ops:
  0.6 0.0 copy-start
  0.6 1.4 %broadcast_in_dim.10 = bf16[4,128,2048]{2,1,0:T(8,128)(2,1)S(1)} broadcast(bf16[128,2048]{1,0:T(8,128)(2,1)} %param.4), dimensions={1,2} | broadcast | bytes 2621440 | tf_op jit(solution)/shard_map/broadcast_in_dim | solution.py:11
  2.1 56.1 %all_to_all.25 = bf16[4,128,2048]{2,1,0:T(8,128)(2,1)} all-to-all(bf16[4,128,2048]{2,1,0:T(8,128)(2,1)S(1)} %broadcast_in_dim.10), channel_id=1, replica_groups=mesh['sensor_0'=2,'sensor_1'=8,'sensor_2'=4,'sensor_3'=2,'batch'=4] {'ba..., dimensions={0} | all-to-all | bytes 4194304 | tf_op jit(solution)/shard_map/all_to_all | solution.py:12
  58.2 4.1 %dot_general.8 = bf16[64,2,4,2048]{3,2,1,0:T(4,128)(2,1)} reshape(bf16[4,128,2048]{2,1,0:T(8,128)(2,1)} %all_to_all.25) | data formatting | bytes 4194304 | tf_op jit(solution)/shard_map/dot_general | solution.py:55
  62.3 0.0 copy-done
  62.3 2.9 %fusion.4 = f32[2,64,4,512]{3,1,2,0:T(8,128)S(1)} fusion(bf16[2048,512]{1,0:T(8,128)(2,1)S(1)} %copy-done, bf16[64,2,4,2048]{3,2,1,0:T(4,128)(2,1)} %dot_general.8), kind=kOutput, calls=%fused_computation.5 | convolution fusion | flops 1073741824 | bytes 5242880 | tf_op jit(solution)/shard_map/dot_general | solution.py:55
  65.2 6.6 %all_to_all.26 = f32[2,64,4,512]{3,1,2,0:T(8,128)S(1)} all-to-all(f32[2,64,4,512]{3,1,2,0:T(8,128)S(1)} %fusion.4), channel_id=1, replica_groups=mesh['sensor_0'=2,'sensor_1'=8,'sensor_2'=4,'sensor_3'=2,'batch'=4] {'se..., dimensions={0} | all-to-all | bytes 2097152 | tf_op jit(solution)/shard_map/all_to_all | solution.py:34
  71.8 0.0 copy-start.1
  71.8 0.0 copy-start.2
  71.8 0.9 reduce_sum.27
  72.7 1.4 copy.14
  74.1 27.2 %all_to_all.27 = f32[64,4,512]{2,1,0:T(4,128)S(1)} all-to-all(f32[64,4,512]{2,1,0:T(4,128)S(1)} %copy.14), channel_id=1, replica_groups=mesh['sensor_0'=2,'sensor_1'=8,'sensor_2'=4,'sensor_3'=2,'batch'=4] {'se..., dimensions={0} | all-to-all | bytes 1048576 | tf_op jit(solution)/shard_map/all_to_all | solution.py:42
  101.3 0.1 reduce_sum.28
  101.4 0.0 copy-done.1
  101.4 0.0 copy-done.2
  101.4 0.6 multiply_convert_fusion
  102.0 0.1 broadcast_in_dim.11
  102.1 20.0 %all_to_all.28 = bf16[64,4,512]{2,1,0:T(4,128)(2,1)S(1)} all-to-all(bf16[64,4,512]{2,1,0:T(4,128)(2,1)S(1)} %broadcast_in_dim.11), channel_id=1, replica_groups=mesh['sensor_0'=2,'sensor_1'=8,'sensor_2'=4,'sensor_3'=2,'batch'=4] {'se..., dimensions={0} | all-to-all | bytes 524288 | tf_op jit(solution)/shard_map/all_to_all | solution.py:12
  122.1 0.1 broadcast_in_dim.12
  122.2 6.7 %all_to_all.29 = bf16[2,64,4,512]{3,2,1,0:T(4,128)(2,1)S(1)} all-to-all(bf16[2,64,4,512]{3,2,1,0:T(4,128)(2,1)S(1)} %broadcast_in_dim.12), channel_id=1, replica_groups=mesh['sensor_0'=2,'sensor_1'=8,'sensor_2'=4,'sensor_3'=2,'batch'=4] {'se..., dimensions={0} | all-to-all | bytes 1048576 | tf_op jit(solution)/shard_map/all_to_all | solution.py:12
  128.9 0.2 copy.15
  129.1 0.9 reshape_reshape.4
  130.0 4.3 %fusion = bf16[2048,512]{0,1:T(8,128)(2,1)} fusion(bf16[512,512]{1,0:T(8,128)(2,1)} %reshape_reshape.4, bf16[512,2048]{1,0:T(8,128)(2,1)} %bitcast.16), kind=kOutput, calls=%fused_computation.1 | convolution fusion | flops 1074790400 | bytes 4718592 | tf_op jit(solution)/shard_map/dot_general | solution.py:62
  134.3 3.9 %copy.16 = bf16[2048,512]{1,0:T(8,128)(2,1)} copy(bf16[2048,512]{0,1:T(8,128)(2,1)} %fusion) | data formatting | bytes 4194304
  138.2 0.9 convert_reduce_fusion
Async XLA Ops:
  0.6 61.6 %copy-start = (bf16[2048,512]{1,0:T(8,128)(2,1)S(1)}, bf16[2048,512]{1,0:T(8,128)(2,1)}, u32[]{:S(2)}) copy-start(bf16[2048,512]{1,0:T(8,128)(2,1)} %param.5) | copy-start | bytes 6291460
  71.8 29.6 %copy-start.1 = (bf16[4,512]{1,0:T(4,128)(2,1)S(1)}, bf16[4,512]{1,0:T(4,128)(2,1)}, u32[]{:S(2)}) copy-start(bf16[4,512]{1,0:T(4,128)(2,1)} %param.7) | copy-start | bytes 12292
  71.8 29.6 %copy-start.2 = (f32[512]{0:T(512)S(1)}, f32[512]{0:T(512)}, u32[]{:S(2)}) copy-start(f32[512]{0:T(512)} %param.6) | copy-start | bytes 6148
where the time goes:
time: 140 us; the launch traced here: 139 us
  blocking collectives  117 us (84%)
  local copies, waits for them, and re-layouts  12.1 us (9%)
  matrix products  7.28 us (5%)
  other arithmetic  2.47 us (2%)
    all_to_all x3, blocking collectives, copy_for_each(): return lax.all_to_all(copies, axis, split_axis=0, concat_axis=0, tiled=True)  82.7 us
    all_to_all x1, blocking collectives, summed_rows(): lax.all_to_all(nearer, far, split_axis=0, concat_axis=0, tiled=True)  27.2 us
    all_to_all x1, blocking collectives, sum_at_owner(): lax.all_to_all(pieces, axis, split_axis=0, concat_axis=0, tiled=True)  6.63 us
    dot_general x1, matrix products, body(): lax.dot_general(all_rows, grad_all, (((0,), (0,)), ((), ())), preferred_e...  4.34 us
    dot_general x1, local copies, waits for them, and re-layouts, body(): jnp.dot(all_rows, branch_weight, preferred_element_type=jnp.float32)  4.09 us
    unnamed x7, local copies, waits for them, and re-layouts  3.93 us
    dot_general x1, matrix products, body(): jnp.dot(all_rows, branch_weight, preferred_element_type=jnp.float32)  2.94 us

commit v1 on v0

v1 whole, which is shorter than its diff:
```python
import jax
import jax.numpy as jnp
from jax import lax
from jax.experimental import pallas as pl
from jax.experimental.pallas import tpu as pltpu
from jax.sharding import Mesh
from jax.sharding import PartitionSpec as P

SENSOR = ("y_lo", "z", "x", "core")
STEPS = 8
ROWS = 32
OWNED = 4
CLASSES = 8
DEPTH = 8
TILE = 256


def group_of(batch, step, half):
    own = step // 2 == 0
    far = step // 2 == 3
    block = jnp.where(own, batch, jnp.where(far, batch + 2, batch + 3 + 2 * half))
    piece = jnp.where(own, 2 * step + half, jnp.where(far, step - 6 + 2 * half, step - 2))
    return lax.rem(block, 4) * 4 + piece


def slot_of(batch, group):
    away = lax.rem(group // 4 + 4 - batch, 4)
    piece = lax.rem(group, 4)
    near = 4 + 2 * piece + jnp.where(away == 1, 1, 0)
    far = 12 + 2 * lax.rem(piece, 2) + piece // 2
    return jnp.where(away == 0, piece, jnp.where(away == 2, far, near))


def kernel(
    samples, weight, bias, upstream,
    act_out, grad_out, bias_out,
    s_buf, w_buf, st_buf, out_buf,
    a_send_buf, a_buf, b_send_buf, b_buf, z_buf, c_buf,
    part, asm, g_buf, u_buf, u_pair, act_buf,
    load_sem, w_sem, u_sem, y_send, y_recv, us_sem, ur_sem, uz_send, uz_recv,
    a_send, a_recv, b_send, b_recv, z_send, z_recv, c_send, c_recv, out_sem,
):
    y_lo, z, x, core = (lax.axis_index(name) for name in SENSOR)
    batch = lax.axis_index("batch")
    mine = 2 * x + core
    up, down = lax.rem(batch + 1, 4), lax.rem(batch + 3, 4)
    other = 1 - y_lo

    def class_peer(d):
        k = lax.rem(mine + d, CLASSES)
        return k, {"x": k // 2, "core": lax.rem(k, 2)}

    def z_peer(d):
        return {"z": lax.rem(z + d, DEPTH)}

    loads = [
        pltpu.make_async_copy(samples.at[pl.ds(ROWS * j, ROWS)], s_buf.at[j], load_sem.at[j]) for j in range(4)
    ]
    for copy in loads:
        copy.start()
    load_w = pltpu.make_async_copy(weight, w_buf, w_sem)
    load_w.start()
    load_u = pltpu.make_async_copy(upstream, u_buf.at[z, y_lo], u_sem)
    load_u.start()

    barrier = pltpu.get_barrier_semaphore()
    for peer in (up, down):
        pl.semaphore_signal(barrier, inc=1, device_id={"batch": peer})
    pl.semaphore_signal(barrier, inc=1, device_id={"y_lo": other})
    for d in range(1, CLASSES):
        pl.semaphore_signal(barrier, inc=1, device_id=class_peer(d)[1])
    for d in range(1, DEPTH):
        pl.semaphore_signal(barrier, inc=1, device_id=z_peer(d))
    for copy in loads:
        copy.wait()
    pl.semaphore_wait(barrier, 3 + CLASSES - 1 + DEPTH - 1)

    def y_copy(source, target, direction, index):
        return pltpu.make_async_remote_copy(
            src_ref=s_buf.at[source],
            dst_ref=s_buf.at[target],
            send_sem=y_send.at[direction, index],
            recv_sem=y_recv.at[target],
            device_id={"batch": up if direction == 0 else down},
        )

    sends = []
    for j in range(4):
        for direction in range(2):
            copy = y_copy(j, 4 + 2 * j + direction, direction, j)
            copy.start()
            sends.append(copy)
    forwards = {}
    for j in range(2):
        forwards[2 + j] = y_copy(4 + 2 * j, 12 + 2 * j, 0, 4 + j)
        forwards[4 + j] = y_copy(4 + 2 * (2 + j) + 1, 12 + 2 * j + 1, 1, 4 + j)

    load_u.wait()
    u_cross = pltpu.make_async_remote_copy(
        src_ref=u_buf.at[z, y_lo], dst_ref=u_buf.at[z, y_lo], send_sem=us_sem, recv_sem=ur_sem,
        device_id={"y_lo": other},
    )
    u_cross.start()
    load_w.wait()

    def spread(source, target, send_sem, recv_sem, peers):
        for device in peers:
            pltpu.make_async_remote_copy(
                src_ref=source, dst_ref=target, send_sem=send_sem, recv_sem=recv_sem, device_id=device
            ).start()

    def await_bytes(region, sem):
        pltpu.make_async_copy(region, region, sem).wait()

    def stage_matmul(p):
        rows = s_buf[pl.ds(2 * p, 2)].reshape(2 * ROWS, s_buf.shape[-1])
        part[...] = jnp.dot(rows, w_buf[...], preferred_element_type=jnp.float32)
        for half in range(2):
            for k in range(CLASSES):
                a_send_buf[p, k, OWNED * half : OWNED * (half + 1), :] = part[
                    ROWS * half + OWNED * k : ROWS * half + OWNED * (k + 1), :
                ]
        for d in range(1, CLASSES):
            k, device = class_peer(d)
            spread(a_send_buf.at[p, k], a_buf.at[p, mine], a_send.at[p], a_recv.at[p], [device])

    def stage_class_sum(p):
        await_bytes(a_buf.at[p, pl.ds(0, CLASSES - 1)], a_recv.at[p])
        total = a_send_buf[p, mine]
        for d in range(1, CLASSES):
            total = total + a_buf[p, lax.rem(mine + d, CLASSES)]
        b_send_buf[p] = total
        spread(b_send_buf.at[p], b_buf.at[p], b_send.at[p], b_recv.at[p], [{"y_lo": other}])

    def stage_pair_sum(p):
        await_bytes(b_buf.at[p], b_recv.at[p])
        z_buf[p, z] = b_send_buf[p] + b_buf[p]
        spread(z_buf.at[p, z], z_buf.at[p, z], z_send.at[p], z_recv.at[p], [z_peer(d) for d in range(1, DEPTH)])

    def stage_gradient(p):
        await_bytes(z_buf.at[p, pl.ds(0, DEPTH - 1)], z_recv.at[p])
        total = z_buf[p, 0]
        for i in range(1, DEPTH):
            total = total + z_buf[p, i]
        act = jnp.tanh(total + bias[...])
        for half in range(2):
            group = group_of(batch, p, half)
            rows = slice(OWNED * half, OWNED * (half + 1))
            u_pair[rows, :] = u_buf[lax.rem(group, DEPTH), group // DEPTH].astype(jnp.float32)
            act_buf[2 * p + half] = act[rows]
        grad = (u_pair[...] * (1.0 - act * act)).astype(jnp.bfloat16).astype(jnp.float32)
        c_buf[p, mine] = grad
        spread(
            c_buf.at[p, mine], c_buf.at[p, mine], c_send.at[p], c_recv.at[p],
            [class_peer(d)[1] for d in range(1, CLASSES)],
        )

    def stage_assemble(p):
        await_bytes(c_buf.at[p, pl.ds(0, CLASSES - 1)], c_recv.at[p])
        for half in range(2):
            for k in range(CLASSES):
                asm[ROWS * half + OWNED * k : ROWS * half + OWNED * (k + 1), :] = c_buf[
                    p, k, OWNED * half : OWNED * (half + 1), :
                ]
        grads = asm[...]
        g_buf[pl.ds(pl.multiple_of(2 * ROWS * p, 2 * ROWS), 2 * ROWS)] = grads.astype(jnp.bfloat16)
        bias_out[...] += jnp.sum(grads, axis=0, keepdims=True)

    def turn(block):
        rows = s_buf[4 * block : 4 * block + 4].reshape(4 * ROWS, s_buf.shape[-1])
        st_buf[:, 4 * ROWS * block : 4 * ROWS * (block + 1)] = rows.T

    bias_out[...] = jnp.zeros_like(bias_out)
    u_cross.wait()
    spread(u_buf.at[z], u_buf.at[z], uz_send, uz_recv, [z_peer(d) for d in range(1, DEPTH)])
    turn(0)

    @pl.loop(0, STEPS + 4)
    def _(s):
        @pl.when(s >= 4)
        def _():
            stage_assemble(s - 4)

        @pl.when(s == 3)
        def _():
            await_bytes(u_buf.at[pl.ds(0, DEPTH - 1)], uz_recv)

        @pl.when((s >= 3) & (s < STEPS + 3))
        def _():
            stage_gradient(s - 3)

        @pl.when((s >= 2) & (s < STEPS + 2))
        def _():
            stage_pair_sum(s - 2)

        @pl.when((s >= 1) & (s < STEPS + 1))
        def _():
            stage_class_sum(s - 1)

        @pl.when(s == 4)
        def _():
            turn(1)

        @pl.when(s == 6)
        def _():
            turn(2)

        for p in range(2, STEPS):
            @pl.when(s == p)
            def _(p=p):
                for half in range(2):
                    y_copy(2 * p + half, 2 * p + half, half, 0).wait_recv()
                if p in forwards:
                    forwards[p].start()

        @pl.when(s < STEPS)
        def _():
            stage_matmul(s)

        @pl.when(s == STEPS - 1)
        def _():
            turn(3)

    act_out[...] = act_buf[slot_of(batch, y_lo * DEPTH + z)].astype(jnp.bfloat16)

    tiles = st_buf.shape[0] // TILE

    def out_copy(t):
        rows = pl.ds(pl.multiple_of(t * TILE, TILE), TILE)
        return pltpu.make_async_copy(out_buf.at[rows], grad_out.at[rows], out_sem.at[t])

    @pl.loop(0, tiles)
    def _(t):
        rows = pl.ds(pl.multiple_of(t * TILE, TILE), TILE)
        out_buf[rows] = jnp.dot(st_buf[rows], g_buf[...], preferred_element_type=jnp.float32).astype(jnp.bfloat16)
        out_copy(t).start()

    for copy in sends:
        copy.wait_send()
    for copy in forwards.values():
        copy.wait_send()
    await_bytes(u_buf.at[pl.ds(0, DEPTH - 1)], uz_send)

    @pl.loop(0, STEPS)
    def _(p):
        await_bytes(a_buf.at[p, pl.ds(0, CLASSES - 1)], a_send.at[p])
        await_bytes(b_buf.at[p], b_send.at[p])
        await_bytes(z_buf.at[p, pl.ds(0, DEPTH - 1)], z_send.at[p])
        await_bytes(c_buf.at[p, pl.ds(0, CLASSES - 1)], c_send.at[p])

    @pl.loop(0, tiles)
    def _(t):
        out_copy(t).wait()


def body(samples, branch_weight, branch_bias, upstream):
    sensors, hidden = branch_weight.shape
    funcs = 4 * samples.shape[0]
    share = 2 * OWNED
    f32, bf16 = jnp.float32, jnp.bfloat16
    dma = pltpu.SemaphoreType.DMA
    tiles = sensors // TILE
    activation, weight_grad, bias_grad = pl.pallas_call(
        kernel,
        out_shape=(
            jax.ShapeDtypeStruct((OWNED, hidden), bf16),
            jax.ShapeDtypeStruct((sensors, hidden), bf16),
            jax.ShapeDtypeStruct((1, hidden), f32),
        ),
        in_specs=[
            pl.BlockSpec(memory_space=pl.ANY),
            pl.BlockSpec(memory_space=pl.ANY),
            pl.BlockSpec(memory_space=pltpu.VMEM),
            pl.BlockSpec(memory_space=pl.ANY),
        ],
        out_specs=(
            pl.BlockSpec(memory_space=pltpu.VMEM),
            pl.BlockSpec(memory_space=pl.ANY),
            pl.BlockSpec(memory_space=pltpu.VMEM),
        ),
        scratch_shapes=[
            pltpu.VMEM((2 * STEPS, ROWS, sensors), bf16),
            pltpu.VMEM((sensors, hidden), bf16),
            pltpu.VMEM((sensors, funcs), bf16),
            pltpu.VMEM((sensors, hidden), bf16),
            pltpu.VMEM((STEPS, CLASSES, share, hidden), f32),
            pltpu.VMEM((STEPS, CLASSES, share, hidden), f32),
            pltpu.VMEM((STEPS, share, hidden), f32),
            pltpu.VMEM((STEPS, share, hidden), f32),
            pltpu.VMEM((STEPS, DEPTH, share, hidden), f32),
            pltpu.VMEM((STEPS, CLASSES, share, hidden), f32),
            pltpu.VMEM((2 * ROWS, hidden), f32),
            pltpu.VMEM((2 * ROWS, hidden), f32),
            pltpu.VMEM((funcs, hidden), bf16),
            pltpu.VMEM((DEPTH, 2, OWNED, hidden), bf16),
            pltpu.VMEM((share, hidden), f32),
            pltpu.VMEM((2 * STEPS, OWNED, hidden), f32),
            dma((4,)), dma, dma, dma((2, 6)), dma((2 * STEPS,)), dma, dma, dma, dma,
            dma((STEPS,)), dma((STEPS,)), dma((STEPS,)), dma((STEPS,)),
            dma((STEPS,)), dma((STEPS,)), dma((STEPS,)), dma((STEPS,)),
            dma((tiles,)),
        ],
        compiler_params=pltpu.CompilerParams(
            collective_id=0, has_side_effects=True, vmem_limit_bytes=48 * 1024 * 1024
        ),
    )(samples, branch_weight, branch_bias[None, :], upstream)
    return activation, weight_grad, bias_grad[0]


def solution(mesh):
    torus = Mesh(
        mesh.devices.reshape(2, 8, 4, 2, mesh.shape["batch"]),
        (*SENSOR, "batch"),
    )
    in_specs = (P("batch", SENSOR), P(SENSOR, "batch"), P("batch"), P(SENSOR, "batch"))
    out_specs = (P(SENSOR, "batch"), P(SENSOR, "batch"), P("batch"))
    return jax.shard_map(body, mesh=torus, in_specs=in_specs, out_specs=out_specs, check_vma=False)
```

time: 140 us -> 108 us (0.77)
  blocking collectives: 117 us -> 0 us
  Pallas kernels: 0 us -> 100 us
  matrix products: 7.28 us -> 0 us
  local copies, waits for them, and re-layouts: 12.1 us -> 6.48 us
  other arithmetic: 2.47 us -> 0 us
    all_to_all x5 -> x0, blocking collectives: 117 us -> none  [the longest x3 82.7 us: copy_for_each(): return lax.all_to_all(copies, axis, split_axis=0, concat_axis=0, tiled=True)]
    pallas_call x0 -> x1, Pallas kernels: none -> 100 us  [body(): pl.pallas_call(kernel, out_shape=(jax.ShapeDtypeStruct((OWNED, hidden), b...]
    dot_general x2 -> x0, matrix products: 7.28 us -> none  [the longest x1 4.34 us: body(): lax.dot_general(all_rows, grad_all, (((0,), (0,)), ((), ())), preferred_e...]
    dot_general x1 -> x0, local copies, waits for them, and re-layouts: 4.09 us -> none  [body(): jnp.dot(all_rows, branch_weight, preferred_element_type=jnp.float32)]
    unnamed x7 -> x11, local copies, waits for them, and re-layouts: 3.93 us -> 6.48 us
    reduce_sum x3 -> x0, other arithmetic: 1.87 us -> none  [the longest x1 0.9 us: sum_at_owner(): return arrived.sum(axis=0)]
    broadcast_in_dim x3 -> x0, local copies, waits for them, and re-layouts: 1.64 us -> none  [copy_for_each(): copies = jnp.broadcast_to(array, (lax.axis_size(axis), *array.shape))]
where the time goes in v1:
time: 108 us; the launch traced here: 107 us
  Pallas kernels  100 us (93%)
  local copies, waits for them, and re-layouts  6.48 us (6%)
    pallas_call x1, Pallas kernels, body(): pl.pallas_call(kernel, out_shape=(jax.ShapeDtypeStruct((OWNED, hidden), b...  100 us
    unnamed x11, local copies, waits for them, and re-layouts  6.48 us

profile of v1, /device:TPU:1, one launch (start us, length us, event | category | flops | bytes accessed | tf_op | source)
XLA Modules:
  0.0 107.3 jit_solution(9416562918450907300)
XLA Ops:
  0.6 0.0 copy-start
  0.6 1.6 %copy-done = bf16[2048,512]{1,0:T(8,128)(2,1)S(1)} copy-done((bf16[2048,512]{1,0:T(8,128)(2,1)S(1)}, bf16[2048,512]{1,0:T(8,128)(2,1)}, u32[]{:S(2)}) %copy-start) | copy-done | bytes 2097176
  2.2 0.0 copy-start.1
  2.2 1.0 copy-done.1
  3.3 0.0 copy-start.2
  3.3 0.7 copy-done.2
  4.0 0.0 copy-start.3
  4.0 0.7 copy-done.3
  4.6 100.1 %shard_map.67 = (bf16[4,512]{1,0:T(4,128)(2,1)S(1)}, bf16[2048,512]{1,0:T(8,128)(2,1)S(1)}, f32[1,512]{1,0:T(1,128)S(1)}) custom-call(bf16[128,2048]{1,0:T(8,128)(2,1)S(1)} %copy-done.1, bf16[2048,512]{1,0:T(8,128)(2,1)S(1)} %copy-done, f32[1,512]{1,0:T(1,128)S(1)} %bitcast.3, bf16[4,512]{1,0:T(4,128)(2,1)S(1)} %copy-done.2), custom_call_target="tpu_custom_call" | custom-call | tf_op jit(solution)/shard_map/pallas_call | solution.py:263
  104.8 0.6 copy.10
  105.4 1.3 %copy.11 = bf16[2048,512]{1,0:T(8,128)(2,1)} copy(bf16[2048,512]{1,0:T(8,128)(2,1)S(1)} %get-tuple-element.13) | data formatting | bytes 4194304
  106.7 0.6 copy.12
Async XLA Ops:
  0.6 1.6 %copy-start = (bf16[2048,512]{1,0:T(8,128)(2,1)S(1)}, bf16[2048,512]{1,0:T(8,128)(2,1)}, u32[]{:S(2)}) copy-start(bf16[2048,512]{1,0:T(8,128)(2,1)} %weight.1) | copy-start | bytes 6291460
  2.2 1.0 copy-start.1
  3.3 0.7 copy-start.2
  4.0 0.7 copy-start.3

commit v2 on v1

v2 whole, which is shorter than its diff:
```python
import jax
import jax.numpy as jnp
from jax import lax
from jax.experimental import pallas as pl
from jax.experimental.pallas import tpu as pltpu
from jax.sharding import Mesh
from jax.sharding import PartitionSpec as P

SENSOR = ("y_lo", "z", "x", "core")
STEPS = 8
ROWS = 32
PIECE = 16
AHEAD = 3
OWNED = 4
CLASSES = 8
DEPTH = 8
TILE = 256


def group_of(batch, step, half):
    own = step // 2 == 0
    far = step // 2 == 3
    block = jnp.where(own, batch, jnp.where(far, batch + 2, batch + 3 + 2 * half))
    piece = jnp.where(own, 2 * step + half, jnp.where(far, step - 6 + 2 * half, step - 2))
    return lax.rem(block, 4) * 4 + piece


def slot_of(batch, group):
    away = lax.rem(group // 4 + 4 - batch, 4)
    piece = lax.rem(group, 4)
    near = 4 + 2 * piece + jnp.where(away == 1, 1, 0)
    far = 12 + 2 * lax.rem(piece, 2) + piece // 2
    return jnp.where(away == 0, piece, jnp.where(away == 2, far, near))


def kernel(
    samples, weight, bias, upstream,
    st_out, g_buf, act_out, bias_out,
    st_buf, s_buf, w_buf, bias_buf,
    a_send_buf, a_buf, b_send_buf, b_buf, z_buf, c_buf,
    part, asm, u_buf, u_pair, act_buf,
    load_sem, w_sem, bias_sem, u_sem, y_send, y_recv, us_sem, ur_sem, uz_send, uz_recv,
    a_send, a_recv, b_send, b_recv, z_send, z_recv, c_send, c_recv, st_sem,
):
    y_lo, z, x, core = (lax.axis_index(name) for name in SENSOR)
    batch = lax.axis_index("batch")
    mine = 2 * x + core
    up, down = lax.rem(batch + 1, 4), lax.rem(batch + 3, 4)
    other = 1 - y_lo

    def class_peer(d):
        k = lax.rem(mine + d, CLASSES)
        return k, {"x": k // 2, "core": lax.rem(k, 2)}

    def z_peer(d):
        return {"z": lax.rem(z + d, DEPTH)}

    loads = [
        pltpu.make_async_copy(samples.at[pl.ds(PIECE * i, PIECE)], s_buf.at[i], load_sem.at[i]) for i in range(8)
    ]
    load_u = pltpu.make_async_copy(upstream, u_buf.at[z, y_lo], u_sem)
    load_w = pltpu.make_async_copy(weight, w_buf, w_sem)
    load_bias = pltpu.make_async_copy(bias, bias_buf, bias_sem)
    load_u.start()
    for copy in loads:
        copy.start()
    load_bias.start()
    load_w.start()

    barrier = pltpu.get_barrier_semaphore()
    for peer in (up, down):
        pl.semaphore_signal(barrier, inc=1, device_id={"batch": peer})
    pl.semaphore_signal(barrier, inc=1, device_id={"y_lo": other})
    for d in range(1, CLASSES):
        pl.semaphore_signal(barrier, inc=1, device_id=class_peer(d)[1])
    for d in range(1, DEPTH):
        pl.semaphore_signal(barrier, inc=1, device_id=z_peer(d))
    load_u.wait()
    for copy in loads:
        copy.wait()
    pl.semaphore_wait(barrier, 3 + CLASSES - 1 + DEPTH - 1)

    u_cross = pltpu.make_async_remote_copy(
        src_ref=u_buf.at[z, y_lo], dst_ref=u_buf.at[z, y_lo], send_sem=us_sem, recv_sem=ur_sem,
        device_id={"y_lo": other},
    )
    u_cross.start()

    def landing(i, direction):
        return 8 + 4 * (i // 2) + 2 * direction + i % 2

    def y_copy(i, direction):
        source = i if i < 8 else landing(i - 8 + 4 * direction, direction)
        target = landing(i, direction)
        return pltpu.make_async_remote_copy(
            src_ref=s_buf.at[source],
            dst_ref=s_buf.at[target],
            send_sem=y_send.at[direction, i],
            recv_sem=y_recv.at[target],
            device_id={"batch": up if direction == 0 else down},
        )

    def y_start(i):
        for direction in range(2):
            y_copy(i, direction).start()

    def y_arrive(i):
        for direction in range(2):
            y_copy(i, direction).wait_recv()
        if i + AHEAD < 12:
            y_start(i + AHEAD)

    for i in range(AHEAD):
        y_start(i)
    load_bias.wait()
    load_w.wait()

    def spread(source, target, send_sem, recv_sem, peers):
        for device in peers:
            pltpu.make_async_remote_copy(
                src_ref=source, dst_ref=target, send_sem=send_sem, recv_sem=recv_sem, device_id=device
            ).start()

    def await_bytes(region, sem):
        pltpu.make_async_copy(region, region, sem).wait()

    def stage_matmul(p):
        rows = s_buf[pl.ds(4 * p, 4)].reshape(2 * ROWS, s_buf.shape[-1])
        part[...] = jnp.dot(rows, w_buf[...], preferred_element_type=jnp.float32)
        for half in range(2):
            for k in range(CLASSES):
                a_send_buf[p, k, OWNED * half : OWNED * (half + 1), :] = part[
                    ROWS * half + OWNED * k : ROWS * half + OWNED * (k + 1), :
                ]
        for d in range(1, CLASSES):
            k, device = class_peer(d)
            spread(a_send_buf.at[p, k], a_buf.at[p, mine], a_send.at[p], a_recv.at[p], [device])

    def stage_class_sum(p):
        await_bytes(a_buf.at[p, pl.ds(0, CLASSES - 1)], a_recv.at[p])
        total = a_send_buf[p, mine]
        for d in range(1, CLASSES):
            total = total + a_buf[p, lax.rem(mine + d, CLASSES)]
        b_send_buf[p] = total
        spread(b_send_buf.at[p], b_buf.at[p], b_send.at[p], b_recv.at[p], [{"y_lo": other}])

    def stage_pair_sum(p):
        await_bytes(b_buf.at[p], b_recv.at[p])
        z_buf[p, z] = b_send_buf[p] + b_buf[p]
        spread(z_buf.at[p, z], z_buf.at[p, z], z_send.at[p], z_recv.at[p], [z_peer(d) for d in range(1, DEPTH)])

    def stage_gradient(p):
        await_bytes(z_buf.at[p, pl.ds(0, DEPTH - 1)], z_recv.at[p])
        total = z_buf[p, 0]
        for i in range(1, DEPTH):
            total = total + z_buf[p, i]
        act = jnp.tanh(total + bias_buf[...][None, :])
        for half in range(2):
            group = group_of(batch, p, half)
            rows = slice(OWNED * half, OWNED * (half + 1))
            u_pair[rows, :] = u_buf[lax.rem(group, DEPTH), group // DEPTH].astype(jnp.float32)
            act_buf[2 * p + half] = act[rows]
        grad = (u_pair[...] * (1.0 - act * act)).astype(jnp.bfloat16).astype(jnp.float32)
        c_buf[p, mine] = grad
        spread(
            c_buf.at[p, mine], c_buf.at[p, mine], c_send.at[p], c_recv.at[p],
            [class_peer(d)[1] for d in range(1, CLASSES)],
        )

    def stage_assemble(p):
        await_bytes(c_buf.at[p, pl.ds(0, CLASSES - 1)], c_recv.at[p])
        for half in range(2):
            for k in range(CLASSES):
                asm[ROWS * half + OWNED * k : ROWS * half + OWNED * (k + 1), :] = c_buf[
                    p, k, OWNED * half : OWNED * (half + 1), :
                ]
        grads = asm[...]
        g_buf[pl.ds(pl.multiple_of(2 * ROWS * p, 2 * ROWS), 2 * ROWS)] = grads.astype(jnp.bfloat16)
        bias_out[...] += jnp.sum(grads, axis=0, keepdims=True)

    def st_copy(block):
        return pltpu.make_async_copy(st_buf.at[block], st_out.at[block], st_sem.at[block])

    def turn(block):
        rows = s_buf[8 * block : 8 * block + 8].reshape(4 * ROWS, s_buf.shape[-1])
        st_buf[block] = rows.T
        st_copy(block).start()

    bias_out[...] = jnp.zeros_like(bias_out)

    def wave(s):
        if 2 <= s < STEPS:
            y_arrive(2 * s - 4)
        if 0 <= s - 5 < STEPS - 2:
            stage_assemble(s - 5)
        if 0 <= s - 4 < STEPS - 2:
            stage_gradient(s - 4)
        if 2 <= s < STEPS:
            y_arrive(2 * s - 3)
        if s < STEPS:
            stage_matmul(s)
        if s == STEPS - 1:
            turn(3)
        if 0 <= s - 3 < STEPS - 2:
            stage_pair_sum(s - 3)
        if 0 <= s - 1 < STEPS:
            stage_class_sum(s - 1)

    wave(0)
    u_cross.wait()
    spread(u_buf.at[z], u_buf.at[z], uz_send, uz_recv, [z_peer(d) for d in range(1, DEPTH)])
    wave(1)
    turn(0)
    wave(2)
    wave(3)
    turn(1)
    await_bytes(u_buf.at[pl.ds(0, DEPTH - 1)], uz_recv)
    wave(4)
    wave(5)
    turn(2)
    wave(6)
    wave(7)
    wave(8)
    last = (STEPS - 2, STEPS - 1)
    for stage in (stage_pair_sum, stage_gradient, stage_assemble):
        if stage is stage_pair_sum:
            wave(9)
        for p in last:
            stage(p)
        if stage is stage_pair_sum:
            wave(10)

    act_out[...] = act_buf[slot_of(batch, y_lo * DEPTH + z)]

    for direction in range(2):
        for i in range(12):
            y_copy(i, direction).wait_send()
    await_bytes(u_buf.at[pl.ds(0, DEPTH - 1)], uz_send)
    for block in range(4):
        st_copy(block).wait()

    @pl.loop(0, STEPS)
    def _(p):
        await_bytes(a_buf.at[p, pl.ds(0, CLASSES - 1)], a_send.at[p])
        await_bytes(b_buf.at[p], b_send.at[p])
        await_bytes(z_buf.at[p, pl.ds(0, DEPTH - 1)], z_send.at[p])
        await_bytes(c_buf.at[p, pl.ds(0, CLASSES - 1)], c_send.at[p])


def weight_kernel(st, g, act, bias, grad_out, act_out, bias_out):
    rows = jnp.concatenate([st[block] for block in range(4)], axis=1)
    grad_out[...] = jnp.dot(rows, g[...], preferred_element_type=jnp.float32).astype(jnp.bfloat16)
    act_out[...] = act[...].astype(jnp.bfloat16)
    bias_out[...] = bias[0]


def body(samples, branch_weight, branch_bias, upstream):
    sensors, hidden = branch_weight.shape
    funcs = 4 * samples.shape[0]
    share = 2 * OWNED
    f32, bf16 = jnp.float32, jnp.bfloat16
    dma = pltpu.SemaphoreType.DMA
    turned, grads, act, bias_sum = pl.pallas_call(
        kernel,
        out_shape=(
            jax.ShapeDtypeStruct((4, sensors, funcs // 4), bf16),
            jax.ShapeDtypeStruct((funcs, hidden), bf16),
            jax.ShapeDtypeStruct((OWNED, hidden), f32),
            jax.ShapeDtypeStruct((1, hidden), f32),
        ),
        in_specs=[pl.BlockSpec(memory_space=pl.ANY)] * 4,
        out_specs=(pl.BlockSpec(memory_space=pl.ANY), *[pl.BlockSpec(memory_space=pltpu.VMEM)] * 3),
        scratch_shapes=[
            pltpu.VMEM((4, sensors, funcs // 4), bf16),
            pltpu.VMEM((32, PIECE, sensors), bf16),
            pltpu.VMEM((sensors, hidden), bf16),
            pltpu.VMEM((hidden,), f32),
            pltpu.VMEM((STEPS, CLASSES, share, hidden), f32),
            pltpu.VMEM((STEPS, CLASSES, share, hidden), f32),
            pltpu.VMEM((STEPS, share, hidden), f32),
            pltpu.VMEM((STEPS, share, hidden), f32),
            pltpu.VMEM((STEPS, DEPTH, share, hidden), f32),
            pltpu.VMEM((STEPS, CLASSES, share, hidden), f32),
            pltpu.VMEM((2 * ROWS, hidden), f32),
            pltpu.VMEM((2 * ROWS, hidden), f32),
            pltpu.VMEM((DEPTH, 2, OWNED, hidden), bf16),
            pltpu.VMEM((share, hidden), f32),
            pltpu.VMEM((2 * STEPS, OWNED, hidden), f32),
            dma((8,)), dma, dma, dma, dma((2, 12)), dma((32,)), dma, dma, dma, dma,
            dma((STEPS,)), dma((STEPS,)), dma((STEPS,)), dma((STEPS,)),
            dma((STEPS,)), dma((STEPS,)), dma((STEPS,)), dma((STEPS,)),
            dma((4,)),
        ],
        compiler_params=pltpu.CompilerParams(
            collective_id=0, has_side_effects=True, vmem_limit_bytes=63 * 1024 * 1024
        ),
    )(samples, branch_weight, branch_bias, upstream)
    whole = lambda *shape: pl.BlockSpec(shape, lambda t: (0,) * len(shape))
    weight_grad, activation, bias_grad = pl.pallas_call(
        weight_kernel,
        grid=(sensors // TILE,),
        out_shape=(
            jax.ShapeDtypeStruct((sensors, hidden), bf16),
            jax.ShapeDtypeStruct((OWNED, hidden), bf16),
            jax.ShapeDtypeStruct((hidden,), f32),
        ),
        in_specs=[pl.BlockSpec((4, TILE, funcs // 4), lambda t: (0, t, 0)), whole(funcs, hidden), whole(OWNED, hidden), whole(1, hidden)],
        out_specs=(pl.BlockSpec((TILE, hidden), lambda t: (t, 0)), whole(OWNED, hidden), whole(hidden)),
    )(turned, grads, act, bias_sum)
    return activation, weight_grad, bias_grad


def solution(mesh):
    torus = Mesh(
        mesh.devices.reshape(2, 8, 4, 2, mesh.shape["batch"]),
        (*SENSOR, "batch"),
    )
    in_specs = (P("batch", SENSOR), P(SENSOR, "batch"), P("batch"), P(SENSOR, "batch"))
    out_specs = (P(SENSOR, "batch"), P(SENSOR, "batch"), P("batch"))
    return jax.shard_map(body, mesh=torus, in_specs=in_specs, out_specs=out_specs, check_vma=False)
```

time: 108 us -> 91.9 us (0.85)
  Pallas kernels: 100 us -> 91 us
  local copies, waits for them, and re-layouts: 6.48 us -> 0 us
    pallas_call x1 -> x2, Pallas kernels: 100 us -> 91 us  [the longest x1 84.1 us: body(): pl.pallas_call(kernel, out_shape=(jax.ShapeDtypeStruct((4, sensors, funcs...]
    unnamed x11 -> x0, local copies, waits for them, and re-layouts: 6.48 us -> none
where the time goes in v2:
time: 91.9 us; the launch traced here: 91.6 us
  Pallas kernels  91 us (99%)
    pallas_call x1, Pallas kernels, body(): pl.pallas_call(kernel, out_shape=(jax.ShapeDtypeStruct((4, sensors, funcs...  84.1 us
    pallas_call x1, Pallas kernels, body(): pl.pallas_call(weight_kernel, grid=(sensors // TILE,), out_shape=(jax.Sha...  6.91 us

profile of v2, /device:TPU:1, one launch (start us, length us, event | category | flops | bytes accessed | tf_op | source)
XLA Modules:
  0.0 91.6 jit_solution(17019858350065350083)
XLA Ops:
  0.6 84.1 %shard_map.67 = (bf16[4,2048,128]{2,1,0:T(8,128)(2,1)}, bf16[512,512]{1,0:T(8,128)(2,1)}, f32[4,512]{1,0:T(4,128)}, f32[1,512]{1,0:T(1,128)}) custom-call(bf16[128,2048]{1,0:T(8,128)(2,1)} %samples.1, bf16[2048,512]{1,0:T(8,128)(2,1)} %weight.1, f32[512]{0:T(512)} %bias.1, bf16[4,512]{1,0:T(4,128)(2,1)} %upstream.1), custom_call_target="tpu_custom_call" | custom-call | tf_op jit(solution)/shard_map/pallas_call | solution.py:263
  84.7 6.9 %shard_map.68 = (bf16[2048,512]{1,0:T(8,128)(2,1)}, bf16[4,512]{1,0:T(4,128)(2,1)}, f32[512]{0:T(512)}) custom-call(bf16[4,2048,128]{2,1,0:T(8,128)(2,1)} %get-tuple-element.10.st, bf16[512,512]{1,0:T(8,128)(2,1)} %get-tuple-element.11.g, f32[4,512]{1,0:T(4,128)} %get-tuple-element.12.act, f32[1,512]{1,0:T(1,128)} %get-tuple-element.13.bias), custom_call_target="tpu_custom_call" | custom-call | tf_op jit(solution)/shard_map/pallas_call | solution.py:299

commit v3 on v2

v3 whole, which is shorter than its diff:
```python
import jax
import jax.numpy as jnp
from jax import lax
from jax.experimental import pallas as pl
from jax.experimental.pallas import tpu as pltpu
from jax.sharding import Mesh
from jax.sharding import PartitionSpec as P

SENSOR = ("y_lo", "z", "x", "core")
STEPS = 10
WIDE = 6
ROWS = 32
PIECE = 16
PIECES = 12
AHEAD = 3
OWNED = 4
CLASSES = 8
DEPTH = 8
TILE = 1024
JOINED = (8, 9)


def halves(p):
    return 2 if p < WIDE else 1


def group_of(batch, p, half):
    if p < 2:
        return batch * 4 + 2 * p + half
    if p < WIDE:
        return lax.rem(batch + 3 + 2 * half, 4) * 4 + p - 2
    return lax.rem(batch + 2, 4) * 4 + p - WIDE


def slot_of(batch, group):
    away = lax.rem(group // 4 + 4 - batch, 4)
    piece = lax.rem(group, 4)
    near = 4 + 2 * piece + jnp.where(away == 1, 1, 0)
    return jnp.where(away == 0, piece, jnp.where(away == 2, 12 + piece, near))


def kernel(
    samples, weight, bias, upstream,
    st_out, g_buf, act_out, bias_out,
    st_buf, s_buf, w_buf, bias_buf,
    a_send_w, a_w, b_send_w, b_w, z_w, c_w,
    a_send_t, a_t, b_send_t, b_t, z_t, c_t,
    part, asm, u_buf, u_pair, act_buf,
    load_sem, w_sem, bias_sem, u_sem, y_send, y_recv, us_sem, ur_sem, uz_send, uz_recv,
    a_send, a_recv, b_send, b_recv, z_send, z_recv, c_send, c_recv, st_sem,
):
    y_lo, z, x, core = (lax.axis_index(name) for name in SENSOR)
    batch = lax.axis_index("batch")
    mine = 2 * x + core
    up, down = lax.rem(batch + 1, 4), lax.rem(batch + 3, 4)
    other = 1 - y_lo

    def class_peer(d):
        k = lax.rem(mine + d, CLASSES)
        return k, {"x": k // 2, "core": lax.rem(k, 2)}

    def z_peer(d):
        return {"z": lax.rem(z + d, DEPTH)}

    place = DEPTH * y_lo + z

    def place_peer(d):
        there = lax.rem(place + d, 2 * DEPTH)
        return {"y_lo": there // DEPTH, "z": lax.rem(there, DEPTH)}

    class_peers = [class_peer(d)[1] for d in range(1, CLASSES)]
    z_peers = [z_peer(d) for d in range(1, DEPTH)]
    place_peers = [place_peer(d) for d in range(1, 2 * DEPTH)]

    loads = [
        pltpu.make_async_copy(samples.at[pl.ds(PIECE * i, PIECE)], s_buf.at[i], load_sem.at[i]) for i in range(8)
    ]
    load_u = pltpu.make_async_copy(upstream, u_buf.at[z, y_lo], u_sem)
    load_w = pltpu.make_async_copy(weight, w_buf, w_sem)
    load_bias = pltpu.make_async_copy(bias, bias_buf, bias_sem)
    load_u.start()
    for copy in loads:
        copy.start()
    load_bias.start()
    load_w.start()

    barrier = pltpu.get_barrier_semaphore()
    for peer in (up, down):
        pl.semaphore_signal(barrier, inc=1, device_id={"batch": peer})
    for device in class_peers + place_peers:
        pl.semaphore_signal(barrier, inc=1, device_id=device)
    load_u.wait()
    for copy in loads:
        copy.wait()
    pl.semaphore_wait(barrier, 2 + CLASSES - 1 + 2 * DEPTH - 1)

    u_cross = pltpu.make_async_remote_copy(
        src_ref=u_buf.at[z, y_lo], dst_ref=u_buf.at[z, y_lo], send_sem=us_sem, recv_sem=ur_sem,
        device_id={"y_lo": other},
    )
    u_cross.start()

    def landing(i, direction):
        return 8 + 4 * (i // 2) + 2 * direction + i % 2 if i < 8 else 24 + 2 * (i - 8) + direction

    def y_copy(i, direction):
        source = i if i < 8 else landing(2 * (i - 8) + direction, direction)
        target = landing(i, direction)
        return pltpu.make_async_remote_copy(
            src_ref=s_buf.at[source],
            dst_ref=s_buf.at[target],
            send_sem=y_send.at[direction, i],
            recv_sem=y_recv.at[target],
            device_id={"batch": up if direction == 0 else down},
        )

    def y_start(i):
        for direction in range(2):
            y_copy(i, direction).start()

    def y_arrive(i):
        for direction in range(2):
            y_copy(i, direction).wait_recv()
        if i + AHEAD < PIECES:
            y_start(i + AHEAD)

    for i in range(AHEAD):
        y_start(i)
    load_bias.wait()
    load_w.wait()

    def spread(source, target, send_sem, recv_sem, peers):
        for device in peers:
            pltpu.make_async_remote_copy(
                src_ref=source, dst_ref=target, send_sem=send_sem, recv_sem=recv_sem, device_id=device
            ).start()

    def await_bytes(region, sem):
        pltpu.make_async_copy(region, region, sem).wait()

    def of(wide, thin, p):
        return wide.at[p] if p < WIDE else thin.at[p - WIDE]

    def stage_matmul(p):
        first, count = (4 * p, 4) if p < WIDE else (24 + 2 * (p - WIDE), 2)
        rows = s_buf[first : first + count].reshape(count * PIECE, s_buf.shape[-1])
        part[: count * PIECE] = jnp.dot(rows, w_buf[...], preferred_element_type=jnp.float32)
        outgoing = of(a_send_w, a_send_t, p)
        for half in range(halves(p)):
            for k in range(CLASSES):
                outgoing[k, OWNED * half : OWNED * (half + 1), :] = part[
                    ROWS * half + OWNED * k : ROWS * half + OWNED * (k + 1), :
                ]
        for d in range(1, CLASSES):
            k, device = class_peer(d)
            spread(outgoing.at[k], of(a_w, a_t, p).at[mine], a_send.at[p], a_recv.at[p], [device])

    def stage_class_sum(p):
        incoming = of(a_w, a_t, p)
        await_bytes(incoming.at[pl.ds(0, CLASSES - 1)], a_recv.at[p])
        total = of(a_send_w, a_send_t, p)[mine]
        for d in range(1, CLASSES):
            total = total + incoming[lax.rem(mine + d, CLASSES)]
        total = total.astype(jnp.bfloat16)
        if p in JOINED:
            shares = of(z_w, z_t, p)
            shares[place] = total
            spread(shares.at[place], shares.at[place], z_send.at[p], z_recv.at[p], place_peers)
        else:
            outgoing = of(b_send_w, b_send_t, p)
            outgoing[...] = total
            spread(outgoing, of(b_w, b_t, p), b_send.at[p], b_recv.at[p], [{"y_lo": other}])

    def stage_pair_sum(p):
        incoming = of(b_w, b_t, p)
        await_bytes(incoming, b_recv.at[p])
        total = of(b_send_w, b_send_t, p)[...].astype(jnp.float32) + incoming[...].astype(jnp.float32)
        shares = of(z_w, z_t, p)
        shares[z] = total.astype(jnp.bfloat16)
        spread(shares.at[z], shares.at[z], z_send.at[p], z_recv.at[p], z_peers)

    def stage_gradient(p):
        shares = of(z_w, z_t, p)
        count = 2 * DEPTH if p in JOINED else DEPTH
        await_bytes(shares.at[pl.ds(0, count - 1)], z_recv.at[p])
        total = shares[0].astype(jnp.float32)
        for i in range(1, count):
            total = total + shares[i].astype(jnp.float32)
        act = jnp.tanh(total + bias_buf[...][None, :])
        for half in range(halves(p)):
            group = group_of(batch, p, half)
            rows = slice(OWNED * half, OWNED * (half + 1))
            u_pair[rows, :] = u_buf[lax.rem(group, DEPTH), group // DEPTH].astype(jnp.float32)
            act_buf[2 * p + half if p < WIDE else p + WIDE] = act[rows]
        scale = u_pair[: OWNED * halves(p)]
        grads = of(c_w, c_t, p)
        grads[mine] = (scale * (1.0 - act * act)).astype(jnp.bfloat16)
        spread(grads.at[mine], grads.at[mine], c_send.at[p], c_recv.at[p], class_peers)

    def stage_assemble(p):
        incoming = of(c_w, c_t, p)
        await_bytes(incoming.at[pl.ds(0, CLASSES - 1)], c_recv.at[p])
        for k in range(CLASSES):
            grads = incoming[k].astype(jnp.float32)
            for half in range(halves(p)):
                asm[ROWS * half + OWNED * k : ROWS * half + OWNED * (k + 1), :] = grads[
                    OWNED * half : OWNED * (half + 1)
                ]
        size = ROWS * halves(p)
        first = 2 * ROWS * p if p < WIDE else ROWS * (p + WIDE)
        grads = asm[:size]
        g_buf[first : first + size] = grads.astype(jnp.bfloat16)
        bias_out[...] += jnp.sum(grads, axis=0, keepdims=True)

    def st_copy(block):
        return pltpu.make_async_copy(st_buf.at[block], st_out.at[block], st_sem.at[block])

    def turn(block):
        rows = s_buf[8 * block : 8 * block + 8].reshape(4 * ROWS, s_buf.shape[-1])
        st_buf[block] = rows.T
        st_copy(block).start()

    bias_out[...] = jnp.zeros_like(bias_out)

    matmul, class_sum, pair_sum, gradient, assemble = (
        stage_matmul, stage_class_sum, stage_pair_sum, stage_gradient, stage_assemble
    )

    matmul(0)
    matmul(1)
    y_arrive(0)
    u_cross.wait()
    spread(u_buf.at[z], u_buf.at[z], uz_send, uz_recv, z_peers)
    y_arrive(1)
    matmul(2)
    class_sum(0)
    class_sum(1)
    y_arrive(2)
    turn(0)
    y_arrive(3)
    matmul(3)
    class_sum(2)
    y_arrive(4)
    pair_sum(0)
    y_arrive(5)
    matmul(4)
    pair_sum(1)
    class_sum(3)
    y_arrive(6)
    pair_sum(2)
    await_bytes(u_buf.at[pl.ds(0, DEPTH - 1)], uz_recv)
    y_arrive(7)
    matmul(5)
    gradient(0)
    class_sum(4)
    turn(1)
    y_arrive(8)
    matmul(6)
    gradient(1)
    pair_sum(3)
    class_sum(5)
    y_arrive(9)
    matmul(7)
    gradient(2)
    assemble(0)
    turn(2)
    class_sum(6)
    y_arrive(10)
    matmul(8)
    pair_sum(4)
    assemble(1)
    class_sum(7)
    y_arrive(11)
    matmul(9)
    pair_sum(5)
    pair_sum(6)
    gradient(3)
    assemble(2)
    class_sum(8)
    pair_sum(7)
    gradient(4)
    turn(3)
    class_sum(9)
    assemble(3)
    gradient(5)
    gradient(6)
    gradient(7)
    gradient(8)
    assemble(4)
    assemble(5)
    gradient(9)
    assemble(6)
    assemble(7)
    assemble(8)
    assemble(9)

    act_out[...] = act_buf[slot_of(batch, y_lo * DEPTH + z)]

    for direction in range(2):
        for i in range(PIECES):
            y_copy(i, direction).wait_send()
    await_bytes(u_buf.at[pl.ds(0, DEPTH - 1)], uz_send)
    for p in range(STEPS):
        await_bytes(of(a_w, a_t, p).at[pl.ds(0, CLASSES - 1)], a_send.at[p])
        if p not in JOINED:
            await_bytes(of(b_w, b_t, p), b_send.at[p])
        count = 2 * DEPTH if p in JOINED else DEPTH
        await_bytes(of(z_w, z_t, p).at[pl.ds(0, count - 1)], z_send.at[p])
        await_bytes(of(c_w, c_t, p).at[pl.ds(0, CLASSES - 1)], c_send.at[p])
    for block in range(4):
        st_copy(block).wait()


def weight_kernel(st, g, act, bias, grad_out, act_out, bias_out):
    rows = jnp.concatenate([st[block] for block in range(4)], axis=1)
    grad_out[...] = jnp.dot(rows, g[...], preferred_element_type=jnp.float32).astype(jnp.bfloat16)
    act_out[...] = act[...].astype(jnp.bfloat16)
    bias_out[...] = bias[0]


def exchange_buffers(steps, rows, places, hidden):
    f32, bf16 = jnp.float32, jnp.bfloat16
    return [
        pltpu.VMEM((steps, CLASSES, rows, hidden), f32),
        pltpu.VMEM((steps, CLASSES, rows, hidden), f32),
        pltpu.VMEM((steps, rows, hidden), bf16),
        pltpu.VMEM((steps, rows, hidden), bf16),
        pltpu.VMEM((steps, places, rows, hidden), bf16),
        pltpu.VMEM((steps, CLASSES, rows, hidden), bf16),
    ]


def body(samples, branch_weight, branch_bias, upstream):
    sensors, hidden = branch_weight.shape
    funcs = 4 * samples.shape[0]
    f32, bf16 = jnp.float32, jnp.bfloat16
    dma = pltpu.SemaphoreType.DMA
    turned, grads, act, bias_sum = pl.pallas_call(
        kernel,
        out_shape=(
            jax.ShapeDtypeStruct((4, sensors, funcs // 4), bf16),
            jax.ShapeDtypeStruct((funcs, hidden), bf16),
            jax.ShapeDtypeStruct((OWNED, hidden), f32),
            jax.ShapeDtypeStruct((1, hidden), f32),
        ),
        in_specs=[pl.BlockSpec(memory_space=pl.ANY)] * 4,
        out_specs=(pl.BlockSpec(memory_space=pl.ANY), *[pl.BlockSpec(memory_space=pltpu.VMEM)] * 3),
        scratch_shapes=[
            pltpu.VMEM((4, sensors, funcs // 4), bf16),
            pltpu.VMEM((32, PIECE, sensors), bf16),
            pltpu.VMEM((sensors, hidden), bf16),
            pltpu.VMEM((hidden,), f32),
            *exchange_buffers(WIDE, 2 * OWNED, DEPTH, hidden),
            *exchange_buffers(STEPS - WIDE, OWNED, 2 * DEPTH, hidden),
            pltpu.VMEM((2 * ROWS, hidden), f32),
            pltpu.VMEM((2 * ROWS, hidden), f32),
            pltpu.VMEM((DEPTH, 2, OWNED, hidden), bf16),
            pltpu.VMEM((2 * OWNED, hidden), f32),
            pltpu.VMEM((16, OWNED, hidden), f32),
            dma((8,)), dma, dma, dma, dma((2, PIECES)), dma((32,)), dma, dma, dma, dma,
            dma((STEPS,)), dma((STEPS,)), dma((STEPS,)), dma((STEPS,)),
            dma((STEPS,)), dma((STEPS,)), dma((STEPS,)), dma((STEPS,)),
            dma((4,)),
        ],
        compiler_params=pltpu.CompilerParams(
            collective_id=0, has_side_effects=True, vmem_limit_bytes=63 * 1024 * 1024
        ),
    )(samples, branch_weight, branch_bias, upstream)
    whole = lambda *shape: pl.BlockSpec(shape, lambda t: (0,) * len(shape))
    weight_grad, activation, bias_grad = pl.pallas_call(
        weight_kernel,
        grid=(sensors // TILE,),
        out_shape=(
            jax.ShapeDtypeStruct((sensors, hidden), bf16),
            jax.ShapeDtypeStruct((OWNED, hidden), bf16),
            jax.ShapeDtypeStruct((hidden,), f32),
        ),
        in_specs=[pl.BlockSpec((4, TILE, funcs // 4), lambda t: (0, t, 0)), whole(funcs, hidden), whole(OWNED, hidden), whole(1, hidden)],
        out_specs=(pl.BlockSpec((TILE, hidden), lambda t: (t, 0)), whole(OWNED, hidden), whole(hidden)),
    )(turned, grads, act, bias_sum)
    return activation, weight_grad, bias_grad


def solution(mesh):
    torus = Mesh(
        mesh.devices.reshape(2, 8, 4, 2, mesh.shape["batch"]),
        (*SENSOR, "batch"),
    )
    in_specs = (P("batch", SENSOR), P(SENSOR, "batch"), P("batch"), P(SENSOR, "batch"))
    out_specs = (P(SENSOR, "batch"), P(SENSOR, "batch"), P("batch"))
    return jax.shard_map(body, mesh=torus, in_specs=in_specs, out_specs=out_specs, check_vma=False)
```

time: 91.9 us -> 74.6 us (0.81)
  Pallas kernels: 91 us -> 73.8 us
    pallas_call x1, Pallas kernels: 84.1 us -> 70 us  [body(): pl.pallas_call(kernel, out_shape=(jax.ShapeDtypeStruct((4, sensors, funcs...]
    pallas_call x1, Pallas kernels: 6.91 us -> 3.82 us  [body(): pl.pallas_call(weight_kernel, grid=(sensors // TILE,), out_shape=(jax.Sha...]
where the time goes in v3:
time: 74.6 us; the launch traced here: 74.4 us
  Pallas kernels  73.8 us (99%)
    pallas_call x1, Pallas kernels, body(): pl.pallas_call(kernel, out_shape=(jax.ShapeDtypeStruct((4, sensors, funcs...  70 us
    pallas_call x1, Pallas kernels, body(): pl.pallas_call(weight_kernel, grid=(sensors // TILE,), out_shape=(jax.Sha...  3.82 us

profile of v3, /device:TPU:1, one launch (start us, length us, event | category | flops | bytes accessed | tf_op | source)
XLA Modules:
  0.0 74.4 jit_solution(11779926066795505495)
XLA Ops:
  0.6 70.0 %shard_map.67 = (bf16[4,2048,128]{2,1,0:T(8,128)(2,1)}, bf16[512,512]{1,0:T(8,128)(2,1)}, f32[4,512]{1,0:T(4,128)}, f32[1,512]{1,0:T(1,128)}) custom-call(bf16[128,2048]{1,0:T(8,128)(2,1)} %samples.1, bf16[2048,512]{1,0:T(8,128)(2,1)} %weight.1, f32[512]{0:T(512)} %bias.1, bf16[4,512]{1,0:T(4,128)(2,1)} %upstream.1), custom_call_target="tpu_custom_call" | custom-call | tf_op jit(solution)/shard_map/pallas_call | solution.py:338
  70.6 3.8 %shard_map.68 = (bf16[2048,512]{1,0:T(8,128)(2,1)}, bf16[4,512]{1,0:T(4,128)(2,1)}, f32[512]{0:T(512)}) custom-call(bf16[4,2048,128]{2,1,0:T(8,128)(2,1)} %get-tuple-element.10.st, bf16[512,512]{1,0:T(8,128)(2,1)} %get-tuple-element.11.g, f32[4,512]{1,0:T(4,128)} %get-tuple-element.12.act, f32[1,512]{1,0:T(1,128)} %get-tuple-element.13.bias), custom_call_target="tpu_custom_call" | custom-call | tf_op jit(solution)/shard_map/pallas_call | solution.py:370

commit v4 on v3

--- a/solution.py
+++ b/solution.py
@@ -44,7 +44,7 @@
     st_out, g_buf, act_out, bias_out,
     st_buf, s_buf, w_buf, bias_buf,
     a_send_w, a_w, b_send_w, b_w, z_w, c_w,
-    a_send_t, a_t, b_send_t, b_t, z_t, c_t,
+    a_send_t, a_t, b_send_t, b_t, z_t, c_t, joined,
     part, asm, u_buf, u_pair, act_buf,
     load_sem, w_sem, bias_sem, u_sem, y_send, y_recv, us_sem, ur_sem, uz_send, uz_recv,
     a_send, a_recv, b_send, b_recv, z_send, z_recv, c_send, c_recv, st_sem,
@@ -161,31 +161,35 @@
         total = of(a_send_w, a_send_t, p)[mine]
         for d in range(1, CLASSES):
             total = total + incoming[lax.rem(mine + d, CLASSES)]
-        total = total.astype(jnp.bfloat16)
         if p in JOINED:
-            shares = of(z_w, z_t, p)
-            shares[place] = total
+            shares = joined.at[p - JOINED[0]]
+            shares[place] = total.astype(jnp.bfloat16)
             spread(shares.at[place], shares.at[place], z_send.at[p], z_recv.at[p], place_peers)
         else:
-            outgoing = of(b_send_w, b_send_t, p)
-            outgoing[...] = total
-            spread(outgoing, of(b_w, b_t, p), b_send.at[p], b_recv.at[p], [{"y_lo": other}])
-
-    def stage_pair_sum(p):
-        incoming = of(b_w, b_t, p)
-        await_bytes(incoming, b_recv.at[p])
-        total = of(b_send_w, b_send_t, p)[...].astype(jnp.float32) + incoming[...].astype(jnp.float32)
-        shares = of(z_w, z_t, p)
-        shares[z] = total.astype(jnp.bfloat16)
-        spread(shares.at[z], shares.at[z], z_send.at[p], z_recv.at[p], z_peers)
-
-    def stage_gradient(p):
-        shares = of(z_w, z_t, p)
-        count = 2 * DEPTH if p in JOINED else DEPTH
+            shares = of(z_w, z_t, p)
+            shares[z] = total
+            spread(shares.at[z], shares.at[z], z_send.at[p], z_recv.at[p], z_peers)
+
+    def sum_shares(shares, p):
+        count = shares.shape[0]
         await_bytes(shares.at[pl.ds(0, count - 1)], z_recv.at[p])
         total = shares[0].astype(jnp.float32)
         for i in range(1, count):
             total = total + shares[i].astype(jnp.float32)
+        return total
+
+    def stage_z_sum(p):
+        outgoing = of(b_send_w, b_send_t, p)
+        outgoing[...] = sum_shares(of(z_w, z_t, p), p).astype(jnp.bfloat16)
+        spread(outgoing, of(b_w, b_t, p), b_send.at[p], b_recv.at[p], [{"y_lo": other}])
+
+    def stage_gradient(p):
+        if p in JOINED:
+            total = sum_shares(joined.at[p - JOINED[0]], p)
+        else:
+            incoming = of(b_w, b_t, p)
+            await_bytes(incoming, b_recv.at[p])
+            total = of(b_send_w, b_send_t, p)[...].astype(jnp.float32) + incoming[...].astype(jnp.float32)
         act = jnp.tanh(total + bias_buf[...][None, :])
         for half in range(halves(p)):
             group = group_of(batch, p, half)
@@ -222,8 +226,8 @@
 
     bias_out[...] = jnp.zeros_like(bias_out)
 
-    matmul, class_sum, pair_sum, gradient, assemble = (
-        stage_matmul, stage_class_sum, stage_pair_sum, stage_gradient, stage_assemble
+    matmul, class_sum, z_sum, gradient, assemble = (
+        stage_matmul, stage_class_sum, stage_z_sum, stage_gradient, stage_assemble
     )
 
     matmul(0)
@@ -241,49 +245,49 @@
     matmul(3)
     class_sum(2)
     y_arrive(4)
-    pair_sum(0)
+    z_sum(0)
     y_arrive(5)
     matmul(4)
-    pair_sum(1)
+    z_sum(1)
     class_sum(3)
     y_arrive(6)
-    pair_sum(2)
+    z_sum(2)
+    turn(1)
     await_bytes(u_buf.at[pl.ds(0, DEPTH - 1)], uz_recv)
     y_arrive(7)
     matmul(5)
+    class_sum(4)
     gradient(0)
-    class_sum(4)
-    turn(1)
     y_arrive(8)
     matmul(6)
+    z_sum(3)
     gradient(1)
-    pair_sum(3)
-    class_sum(5)
     y_arrive(9)
     matmul(7)
+    class_sum(5)
+    assemble(0)
     gradient(2)
-    assemble(0)
-    turn(2)
     class_sum(6)
     y_arrive(10)
     matmul(8)
-    pair_sum(4)
+    z_sum(4)
     assemble(1)
+    turn(2)
     class_sum(7)
     y_arrive(11)
     matmul(9)
-    pair_sum(5)
-    pair_sum(6)
     gradient(3)
+    z_sum(5)
+    class_sum(8)
+    z_sum(6)
     assemble(2)
-    class_sum(8)
-    pair_sum(7)
     gradient(4)
     turn(3)
     class_sum(9)
-    assemble(3)
+    z_sum(7)
     gradient(5)
     gradient(6)
+    assemble(3)
     gradient(7)
     gradient(8)
     assemble(4)
@@ -302,10 +306,11 @@
     await_bytes(u_buf.at[pl.ds(0, DEPTH - 1)], uz_send)
     for p in range(STEPS):
         await_bytes(of(a_w, a_t, p).at[pl.ds(0, CLASSES - 1)], a_send.at[p])
-        if p not in JOINED:
+        if p in JOINED:
+            await_bytes(joined.at[p - JOINED[0], pl.ds(0, 2 * DEPTH - 1)], z_send.at[p])
+        else:
+            await_bytes(of(z_w, z_t, p).at[pl.ds(0, DEPTH - 1)], z_send.at[p])
             await_bytes(of(b_w, b_t, p), b_send.at[p])
-        count = 2 * DEPTH if p in JOINED else DEPTH
-        await_bytes(of(z_w, z_t, p).at[pl.ds(0, count - 1)], z_send.at[p])
         await_bytes(of(c_w, c_t, p).at[pl.ds(0, CLASSES - 1)], c_send.at[p])
     for block in range(4):
         st_copy(block).wait()
@@ -318,14 +323,14 @@
     bias_out[...] = bias[0]
 
 
-def exchange_buffers(steps, rows, places, hidden):
+def exchange_buffers(steps, rows, hidden):
     f32, bf16 = jnp.float32, jnp.bfloat16
     return [
         pltpu.VMEM((steps, CLASSES, rows, hidden), f32),
         pltpu.VMEM((steps, CLASSES, rows, hidden), f32),
         pltpu.VMEM((steps, rows, hidden), bf16),
         pltpu.VMEM((steps, rows, hidden), bf16),
-        pltpu.VMEM((steps, places, rows, hidden), bf16),
+        pltpu.VMEM((steps, DEPTH, rows, hidden), f32),
         pltpu.VMEM((steps, CLASSES, rows, hidden), bf16),
     ]
 
@@ -350,8 +355,9 @@
             pltpu.VMEM((32, PIECE, sensors), bf16),
             pltpu.VMEM((sensors, hidden), bf16),
             pltpu.VMEM((hidden,), f32),
-            *exchange_buffers(WIDE, 2 * OWNED, DEPTH, hidden),
-            *exchange_buffers(STEPS - WIDE, OWNED, 2 * DEPTH, hidden),
+            *exchange_buffers(WIDE, 2 * OWNED, hidden),
+            *exchange_buffers(STEPS - WIDE, OWNED, hidden),
+            pltpu.VMEM((len(JOINED), 2 * DEPTH, OWNED, hidden), bf16),
             pltpu.VMEM((2 * ROWS, hidden), f32),
             pltpu.VMEM((2 * ROWS, hidden), f32),
             pltpu.VMEM((DEPTH, 2, OWNED, hidden), bf16),

time: 74.6 us -> 72.3 us (0.969)
  Pallas kernels: 73.8 us -> 71.5 us
    pallas_call x1, Pallas kernels: 70 us -> 67.7 us  [body(): pl.pallas_call(kernel, out_shape=(jax.ShapeDtypeStruct((4, sensors, funcs...]
where the time goes in v4:
time: 72.3 us; the launch traced here: 72.2 us
  Pallas kernels  71.5 us (99%)
    pallas_call x1, Pallas kernels, body(): pl.pallas_call(kernel, out_shape=(jax.ShapeDtypeStruct((4, sensors, funcs...  67.7 us
    pallas_call x1, Pallas kernels, body(): pl.pallas_call(weight_kernel, grid=(sensors // TILE,), out_shape=(jax.Sha...  3.81 us

profile of v4, /device:TPU:1, one launch (start us, length us, event | category | flops | bytes accessed | tf_op | source)
XLA Modules:
  0.0 72.2 jit_solution(16455607667870879174)
XLA Ops:
  0.6 67.7 %shard_map.67 = (bf16[4,2048,128]{2,1,0:T(8,128)(2,1)}, bf16[512,512]{1,0:T(8,128)(2,1)}, f32[4,512]{1,0:T(4,128)}, f32[1,512]{1,0:T(1,128)}) custom-call(bf16[128,2048]{1,0:T(8,128)(2,1)} %samples.1, bf16[2048,512]{1,0:T(8,128)(2,1)} %weight.1, f32[512]{0:T(512)} %bias.1, bf16[4,512]{1,0:T(4,128)(2,1)} %upstream.1), custom_call_target="tpu_custom_call" | custom-call | tf_op jit(solution)/shard_map/pallas_call | solution.py:343
  68.3 3.8 %shard_map.68 = (bf16[2048,512]{1,0:T(8,128)(2,1)}, bf16[4,512]{1,0:T(4,128)(2,1)}, f32[512]{0:T(512)}) custom-call(bf16[4,2048,128]{2,1,0:T(8,128)(2,1)} %get-tuple-element.10.st, bf16[512,512]{1,0:T(8,128)(2,1)} %get-tuple-element.11.g, f32[4,512]{1,0:T(4,128)} %get-tuple-element.12.act, f32[1,512]{1,0:T(1,128)} %get-tuple-element.13.bias), custom_call_target="tpu_custom_call" | custom-call | tf_op jit(solution)/shard_map/pallas_call | solution.py:376

commit v5 on v4

--- a/solution.py
+++ b/solution.py
@@ -41,13 +41,13 @@
 
 def kernel(
     samples, weight, bias, upstream,
-    st_out, g_buf, act_out, bias_out,
-    st_buf, s_buf, w_buf, bias_buf,
+    st_out, early_out, g_out, act_out, bias_out,
+    st_buf, early_buf, g_buf, s_buf, w_buf, bias_buf,
     a_send_w, a_w, b_send_w, b_w, z_w, c_w,
     a_send_t, a_t, b_send_t, b_t, z_t, c_t, joined,
     part, asm, u_buf, u_pair, act_buf,
     load_sem, w_sem, bias_sem, u_sem, y_send, y_recv, us_sem, ur_sem, uz_send, uz_recv,
-    a_send, a_recv, b_send, b_recv, z_send, z_recv, c_send, c_recv, st_sem,
+    a_send, a_recv, b_send, b_recv, z_send, z_recv, c_send, c_recv, st_sem, early_sem, near_sem,
 ):
     y_lo, z, x, core = (lax.axis_index(name) for name in SENSOR)
     batch = lax.axis_index("batch")
@@ -85,14 +85,25 @@
     load_w.start()
 
     barrier = pltpu.get_barrier_semaphore()
-    for peer in (up, down):
-        pl.semaphore_signal(barrier, inc=1, device_id={"batch": peer})
-    for device in class_peers + place_peers:
+    near = [
+        {"core": 1 - core},
+        {"x": lax.rem(x + 1, 4)},
+        {"x": lax.rem(x + 3, 4)},
+        {"z": lax.rem(z + 1, DEPTH)},
+        {"z": lax.rem(z + DEPTH - 1, DEPTH)},
+        {"y_lo": other},
+    ]
+    for device in [{"batch": up}, {"batch": down}, *near]:
         pl.semaphore_signal(barrier, inc=1, device_id=device)
+
+    def hear_further(r):
+        for device in near:
+            pl.semaphore_signal(near_sem.at[r], inc=1, device_id=device)
+        pl.semaphore_wait(near_sem.at[r], len(near))
     load_u.wait()
     for copy in loads:
         copy.wait()
-    pl.semaphore_wait(barrier, 2 + CLASSES - 1 + 2 * DEPTH - 1)
+    pl.semaphore_wait(barrier, 2 + len(near))
 
     u_cross = pltpu.make_async_remote_copy(
         src_ref=u_buf.at[z, y_lo], dst_ref=u_buf.at[z, y_lo], send_sem=us_sem, recv_sem=ur_sem,
@@ -213,16 +224,32 @@
         size = ROWS * halves(p)
         first = 2 * ROWS * p if p < WIDE else ROWS * (p + WIDE)
         grads = asm[:size]
-        g_buf[first : first + size] = grads.astype(jnp.bfloat16)
+        late = 4 * ROWS * 2
+        if first < late:
+            g_buf[first : first + size] = grads.astype(jnp.bfloat16)
+        else:
+            g_out[first - late : first - late + size] = grads.astype(jnp.bfloat16)
         bias_out[...] += jnp.sum(grads, axis=0, keepdims=True)
 
     def st_copy(block):
-        return pltpu.make_async_copy(st_buf.at[block], st_out.at[block], st_sem.at[block])
+        return pltpu.make_async_copy(st_buf.at[block], st_out.at[block - 2], st_sem.at[block - 2])
 
     def turn(block):
         rows = s_buf[8 * block : 8 * block + 8].reshape(4 * ROWS, s_buf.shape[-1])
         st_buf[block] = rows.T
-        st_copy(block).start()
+        if block >= 2:
+            st_copy(block).start()
+
+    def early_copy(t):
+        rows = pl.ds(TILE * t, TILE)
+        return pltpu.make_async_copy(early_buf.at[rows], early_out.at[rows], early_sem.at[t])
+
+    def early_gradient():
+        for t in range(early_buf.shape[0] // TILE):
+            rows = pl.ds(TILE * t, TILE)
+            turned = jnp.concatenate([st_buf[block, rows] for block in range(2)], axis=1)
+            early_buf[rows] = jnp.dot(turned, g_buf[...], preferred_element_type=jnp.float32).astype(jnp.bfloat16)
+            early_copy(t).start()
 
     bias_out[...] = jnp.zeros_like(bias_out)
 
@@ -230,9 +257,13 @@
         stage_matmul, stage_class_sum, stage_z_sum, stage_gradient, stage_assemble
     )
 
+    hear_further(0)
+    hear_further(1)
     matmul(0)
+    hear_further(2)
     matmul(1)
     y_arrive(0)
+    hear_further(3)
     u_cross.wait()
     spread(u_buf.at[z], u_buf.at[z], uz_send, uz_recv, z_peers)
     y_arrive(1)
@@ -290,6 +321,7 @@
     assemble(3)
     gradient(7)
     gradient(8)
+    early_gradient()
     assemble(4)
     assemble(5)
     gradient(9)
@@ -312,13 +344,16 @@
             await_bytes(of(z_w, z_t, p).at[pl.ds(0, DEPTH - 1)], z_send.at[p])
             await_bytes(of(b_w, b_t, p), b_send.at[p])
         await_bytes(of(c_w, c_t, p).at[pl.ds(0, CLASSES - 1)], c_send.at[p])
-    for block in range(4):
+    for block in range(2, 4):
         st_copy(block).wait()
-
-
-def weight_kernel(st, g, act, bias, grad_out, act_out, bias_out):
-    rows = jnp.concatenate([st[block] for block in range(4)], axis=1)
-    grad_out[...] = jnp.dot(rows, g[...], preferred_element_type=jnp.float32).astype(jnp.bfloat16)
+    for t in range(early_buf.shape[0] // TILE):
+        early_copy(t).wait()
+
+
+def weight_kernel(st, early, g, act, bias, grad_out, act_out, bias_out):
+    rows = jnp.concatenate([st[block] for block in range(2)], axis=1)
+    late = jnp.dot(rows, g[...], preferred_element_type=jnp.float32)
+    grad_out[...] = (early[...].astype(jnp.float32) + late).astype(jnp.bfloat16)
     act_out[...] = act[...].astype(jnp.bfloat16)
     bias_out[...] = bias[0]
 
@@ -340,18 +375,21 @@
     funcs = 4 * samples.shape[0]
     f32, bf16 = jnp.float32, jnp.bfloat16
     dma = pltpu.SemaphoreType.DMA
-    turned, grads, act, bias_sum = pl.pallas_call(
+    turned, early, grads, act, bias_sum = pl.pallas_call(
         kernel,
         out_shape=(
-            jax.ShapeDtypeStruct((4, sensors, funcs // 4), bf16),
-            jax.ShapeDtypeStruct((funcs, hidden), bf16),
+            jax.ShapeDtypeStruct((2, sensors, funcs // 4), bf16),
+            jax.ShapeDtypeStruct((sensors, hidden), bf16),
+            jax.ShapeDtypeStruct((funcs // 2, hidden), bf16),
             jax.ShapeDtypeStruct((OWNED, hidden), f32),
             jax.ShapeDtypeStruct((1, hidden), f32),
         ),
         in_specs=[pl.BlockSpec(memory_space=pl.ANY)] * 4,
-        out_specs=(pl.BlockSpec(memory_space=pl.ANY), *[pl.BlockSpec(memory_space=pltpu.VMEM)] * 3),
+        out_specs=(*[pl.BlockSpec(memory_space=pl.ANY)] * 2, *[pl.BlockSpec(memory_space=pltpu.VMEM)] * 3),
         scratch_shapes=[
             pltpu.VMEM((4, sensors, funcs // 4), bf16),
+            pltpu.VMEM((sensors, hidden), bf16),
+            pltpu.VMEM((funcs // 2, hidden), bf16),
             pltpu.VMEM((32, PIECE, sensors), bf16),
             pltpu.VMEM((sensors, hidden), bf16),
             pltpu.VMEM((hidden,), f32),
@@ -366,7 +404,8 @@
             dma((8,)), dma, dma, dma, dma((2, PIECES)), dma((32,)), dma, dma, dma, dma,
             dma((STEPS,)), dma((STEPS,)), dma((STEPS,)), dma((STEPS,)),
             dma((STEPS,)), dma((STEPS,)), dma((STEPS,)), dma((STEPS,)),
-            dma((4,)),
+            dma((2,)), dma((sensors // TILE,)),
+            pltpu.SemaphoreType.REGULAR((4,)),
         ],
         compiler_params=pltpu.CompilerParams(
             collective_id=0, has_side_effects=True, vmem_limit_bytes=63 * 1024 * 1024
@@ -381,9 +420,13 @@
             jax.ShapeDtypeStruct((OWNED, hidden), bf16),
             jax.ShapeDtypeStruct((hidden,), f32),
         ),
-        in_specs=[pl.BlockSpec((4, TILE, funcs // 4), lambda t: (0, t, 0)), whole(funcs, hidden), whole(OWNED, hidden), whole(1, hidden)],
+        in_specs=[
+            pl.BlockSpec((2, TILE, funcs // 4), lambda t: (0, t, 0)),
+            pl.BlockSpec((TILE, hidden), lambda t: (t, 0)),
+            whole(funcs // 2, hidden),
+            whole(OWNED, hidden), whole(1, hidden)],
         out_specs=(pl.BlockSpec((TILE, hidden), lambda t: (t, 0)), whole(OWNED, hidden), whole(hidden)),
-    )(turned, grads, act, bias_sum)
+    )(turned, early, grads, act, bias_sum)
     return activation, weight_grad, bias_grad
 
 

time: 72.3 us -> 71.6 us (level)
  no operation moved by 1% of the time
where the time goes in v5:
time: 71.6 us; the launch traced here: 71.4 us
  Pallas kernels  70.8 us (99%)
    pallas_call x1, Pallas kernels, body(): pl.pallas_call(kernel, out_shape=(jax.ShapeDtypeStruct((2, sensors, funcs...  67.4 us
    pallas_call x1, Pallas kernels, body(): pl.pallas_call(weight_kernel, grid=(sensors // TILE,), out_shape=(jax.Sha...  3.41 us

profile of v5, /device:TPU:1, one launch (start us, length us, event | category | flops | bytes accessed | tf_op | source)
XLA Modules:
  0.0 71.4 jit_solution(18259873091184696753)
XLA Ops:
  0.6 67.4 %shard_map.67 = (bf16[2,2048,128]{2,1,0:T(8,128)(2,1)}, bf16[2048,512]{1,0:T(8,128)(2,1)}, bf16[256,512]{1,0:T(8,128)(2,1)}, f32[4,512]{1,0:T(4,128)}, f32[1,512]{1,0:T(1,128)}) custom-call(bf16[128,2048]{1,0:T(8,128)(2,1)} %samples.1, bf16[2048,512]{1,0:T(8,128)(2,1)} %weight.1, f32[512]{0:T(512)} %bias.1, bf16[4,512]{1,0:T(4,128)(2,1)} %upstream.1), custom_call_target="tpu_custom_call" | custom-call | tf_op jit(solution)/shard_map/pallas_call | solution.py:378
  68.0 3.4 %shard_map.68 = (bf16[2048,512]{1,0:T(8,128)(2,1)}, bf16[4,512]{1,0:T(4,128)(2,1)}, f32[512]{0:T(512)}) custom-call(bf16[2,2048,128]{2,1,0:T(8,128)(2,1)} %get-tuple-element.11.st, bf16[2048,512]{1,0:T(8,128)(2,1)} %get-tuple-element.12.early, bf16[256,512]{1,0:T(8,128)(2,1)} %get-tuple-element.13.g, f32[4,512]{1,0:T(4,128)} %get-tuple-element.14.act, ...), custom_call_target="tpu_custom_call" | custom-call | tf_op jit(solution)/shard_map/pallas_call | solution.py:415

commit v6 on v5

--- a/solution.py
+++ b/solution.py
@@ -17,6 +17,7 @@
 CLASSES = 8
 DEPTH = 8
 TILE = 1024
+WEIGHT_TILES = 4
 JOINED = (8, 9)
 
 
@@ -101,7 +102,7 @@
             pl.semaphore_signal(near_sem.at[r], inc=1, device_id=device)
         pl.semaphore_wait(near_sem.at[r], len(near))
     load_u.wait()
-    for copy in loads:
+    for copy in loads[:AHEAD]:
         copy.wait()
     pl.semaphore_wait(barrier, 2 + len(near))
 
@@ -137,6 +138,8 @@
 
     for i in range(AHEAD):
         y_start(i)
+    for copy in loads[AHEAD:]:
+        copy.wait()
     load_bias.wait()
     load_w.wait()
 
@@ -319,9 +322,9 @@
     gradient(5)
     gradient(6)
     assemble(3)
+    early_gradient()
     gradient(7)
     gradient(8)
-    early_gradient()
     assemble(4)
     assemble(5)
     gradient(9)
@@ -350,12 +353,46 @@
         early_copy(t).wait()
 
 
-def weight_kernel(st, early, g, act, bias, grad_out, act_out, bias_out):
-    rows = jnp.concatenate([st[block] for block in range(2)], axis=1)
-    late = jnp.dot(rows, g[...], preferred_element_type=jnp.float32)
-    grad_out[...] = (early[...].astype(jnp.float32) + late).astype(jnp.bfloat16)
-    act_out[...] = act[...].astype(jnp.bfloat16)
-    bias_out[...] = bias[0]
+def weight_kernel(
+    st, early, g, act, bias, grad_out, act_out, bias_out,
+    st_buf, early_buf, g_buf, act_buf, bias_buf, out_buf, load_sem, small_sem, out_sem,
+):
+    tiles, _, tile, _ = st_buf.shape
+    load_g = pltpu.make_async_copy(g, g_buf, small_sem.at[0])
+    load_g.start()
+    loads = []
+    for t in range(tiles):
+        rows = pl.ds(tile * t, tile)
+        loads.append((
+            pltpu.make_async_copy(st.at[:, rows], st_buf.at[t], load_sem.at[0, t]),
+            pltpu.make_async_copy(early.at[rows], early_buf.at[t], load_sem.at[1, t]),
+        ))
+        for copy in loads[t]:
+            copy.start()
+    small = [
+        pltpu.make_async_copy(act, act_buf, small_sem.at[1]),
+        pltpu.make_async_copy(bias, bias_buf, small_sem.at[2]),
+    ]
+    for copy in small:
+        copy.start()
+    load_g.wait()
+    stores = []
+    for t in range(tiles):
+        for copy in loads[t]:
+            copy.wait()
+        rows = jnp.concatenate([st_buf[t, block] for block in range(2)], axis=1)
+        late = jnp.dot(rows, g_buf[...], preferred_element_type=jnp.float32)
+        out_buf[t] = (early_buf[t].astype(jnp.float32) + late).astype(jnp.bfloat16)
+        store = pltpu.make_async_copy(out_buf.at[t], grad_out.at[pl.ds(tile * t, tile)], out_sem.at[t])
+        store.start()
+        stores.append(store)
+        if t == 0:
+            for copy in small:
+                copy.wait()
+            act_out[...] = act_buf[...].astype(jnp.bfloat16)
+            bias_out[...] = bias_buf[0]
+    for store in stores:
+        store.wait()
 
 
 def exchange_buffers(steps, rows, hidden):
@@ -411,21 +448,26 @@
             collective_id=0, has_side_effects=True, vmem_limit_bytes=63 * 1024 * 1024
         ),
     )(samples, branch_weight, branch_bias, upstream)
-    whole = lambda *shape: pl.BlockSpec(shape, lambda t: (0,) * len(shape))
+    tile = sensors // WEIGHT_TILES
     weight_grad, activation, bias_grad = pl.pallas_call(
         weight_kernel,
-        grid=(sensors // TILE,),
         out_shape=(
             jax.ShapeDtypeStruct((sensors, hidden), bf16),
             jax.ShapeDtypeStruct((OWNED, hidden), bf16),
             jax.ShapeDtypeStruct((hidden,), f32),
         ),
-        in_specs=[
-            pl.BlockSpec((2, TILE, funcs // 4), lambda t: (0, t, 0)),
-            pl.BlockSpec((TILE, hidden), lambda t: (t, 0)),
-            whole(funcs // 2, hidden),
-            whole(OWNED, hidden), whole(1, hidden)],
-        out_specs=(pl.BlockSpec((TILE, hidden), lambda t: (t, 0)), whole(OWNED, hidden), whole(hidden)),
+        in_specs=[pl.BlockSpec(memory_space=pl.ANY)] * 5,
+        out_specs=(pl.BlockSpec(memory_space=pl.ANY), *[pl.BlockSpec(memory_space=pltpu.VMEM)] * 2),
+        scratch_shapes=[
+            pltpu.VMEM((WEIGHT_TILES, 2, tile, funcs // 4), bf16),
+            pltpu.VMEM((WEIGHT_TILES, tile, hidden), bf16),
+            pltpu.VMEM((funcs // 2, hidden), bf16),
+            pltpu.VMEM((OWNED, hidden), f32),
+            pltpu.VMEM((1, hidden), f32),
+            pltpu.VMEM((WEIGHT_TILES, tile, hidden), bf16),
+            dma((2, WEIGHT_TILES)), dma((3,)), dma((WEIGHT_TILES,)),
+        ],
+        compiler_params=pltpu.CompilerParams(vmem_limit_bytes=63 * 1024 * 1024),
     )(turned, early, grads, act, bias_sum)
     return activation, weight_grad, bias_grad
 

time: 71.6 us -> 72.7 us (1.015)
  Pallas kernels: 70.8 us -> 71.9 us
    pallas_call x1, Pallas kernels: 3.41 us -> 4.22 us  [body(): pl.pallas_call(weight_kernel, out_shape=(jax.ShapeDtypeStruct((sensors, h...]
where the time goes in v6:
time: 72.7 us; the launch traced here: 72.6 us
  Pallas kernels  71.9 us (99%)
    pallas_call x1, Pallas kernels, body(): pl.pallas_call(kernel, out_shape=(jax.ShapeDtypeStruct((2, sensors, funcs...  67.7 us
    pallas_call x1, Pallas kernels, body(): pl.pallas_call(weight_kernel, out_shape=(jax.ShapeDtypeStruct((sensors, h...  4.22 us

profile of v6, /device:TPU:1, one launch (start us, length us, event | category | flops | bytes accessed | tf_op | source)
XLA Modules:
  0.0 72.6 jit_solution(2090764246883269147)
XLA Ops:
  0.6 67.7 %shard_map.67 = (bf16[2,2048,128]{2,1,0:T(8,128)(2,1)}, bf16[2048,512]{1,0:T(8,128)(2,1)}, bf16[256,512]{1,0:T(8,128)(2,1)}, f32[4,512]{1,0:T(4,128)}, f32[1,512]{1,0:T(1,128)}) custom-call(bf16[128,2048]{1,0:T(8,128)(2,1)} %samples.1, bf16[2048,512]{1,0:T(8,128)(2,1)} %weight.1, f32[512]{0:T(512)} %bias.1, bf16[4,512]{1,0:T(4,128)(2,1)} %upstream.1), custom_call_target="tpu_custom_call" | custom-call | tf_op jit(solution)/shard_map/pallas_call | solution.py:415
  68.4 4.2 %shard_map.68 = (bf16[2048,512]{1,0:T(8,128)(2,1)}, bf16[4,512]{1,0:T(4,128)(2,1)}, f32[512]{0:T(512)}) custom-call(bf16[2,2048,128]{2,1,0:T(8,128)(2,1)} %get-tuple-element.11.st, bf16[2048,512]{1,0:T(8,128)(2,1)} %get-tuple-element.12.early, bf16[256,512]{1,0:T(8,128)(2,1)} %get-tuple-element.13.g, f32[4,512]{1,0:T(4,128)} %get-tuple-element.14.act, ...), custom_call_target="tpu_custom_call" | custom-call | tf_op jit(solution)/shard_map/pallas_call | solution.py:452

commit v7 on v5

--- a/solution.py
+++ b/solution.py
@@ -321,10 +321,10 @@
     assemble(3)
     gradient(7)
     gradient(8)
-    early_gradient()
     assemble(4)
     assemble(5)
     gradient(9)
+    early_gradient()
     assemble(6)
     assemble(7)
     assemble(8)

time: 71.6 us -> 71.6 us (level)
  no operation moved by 1% of the time
where the time goes in v7:
time: 71.6 us; the launch traced here: 71.4 us
  Pallas kernels  70.8 us (99%)
    pallas_call x1, Pallas kernels, body(): pl.pallas_call(kernel, out_shape=(jax.ShapeDtypeStruct((2, sensors, funcs...  67.4 us
    pallas_call x1, Pallas kernels, body(): pl.pallas_call(weight_kernel, grid=(sensors // TILE,), out_shape=(jax.Sha...  3.41 us

profile of v7, /device:TPU:1, one launch (start us, length us, event | category | flops | bytes accessed | tf_op | source)
XLA Modules:
  0.0 71.4 jit_solution(15564074952003948624)
XLA Ops:
  0.6 67.4 %shard_map.67 = (bf16[2,2048,128]{2,1,0:T(8,128)(2,1)}, bf16[2048,512]{1,0:T(8,128)(2,1)}, bf16[256,512]{1,0:T(8,128)(2,1)}, f32[4,512]{1,0:T(4,128)}, f32[1,512]{1,0:T(1,128)}) custom-call(bf16[128,2048]{1,0:T(8,128)(2,1)} %samples.1, bf16[2048,512]{1,0:T(8,128)(2,1)} %weight.1, f32[512]{0:T(512)} %bias.1, bf16[4,512]{1,0:T(4,128)(2,1)} %upstream.1), custom_call_target="tpu_custom_call" | custom-call | tf_op jit(solution)/shard_map/pallas_call | solution.py:378
  68.0 3.4 %shard_map.68 = (bf16[2048,512]{1,0:T(8,128)(2,1)}, bf16[4,512]{1,0:T(4,128)(2,1)}, f32[512]{0:T(512)}) custom-call(bf16[2,2048,128]{2,1,0:T(8,128)(2,1)} %get-tuple-element.11.st, bf16[2048,512]{1,0:T(8,128)(2,1)} %get-tuple-element.12.early, bf16[256,512]{1,0:T(8,128)(2,1)} %get-tuple-element.13.g, f32[4,512]{1,0:T(4,128)} %get-tuple-element.14.act, ...), custom_call_target="tpu_custom_call" | custom-call | tf_op jit(solution)/shard_map/pallas_call | solution.py:415

commit v8 on v7

--- a/solution.py
+++ b/solution.py
@@ -307,24 +307,24 @@
     class_sum(7)
     y_arrive(11)
     matmul(9)
-    gradient(3)
     z_sum(5)
     class_sum(8)
     z_sum(6)
     assemble(2)
-    gradient(4)
     turn(3)
     class_sum(9)
     z_sum(7)
+    gradient(3)
+    gradient(4)
     gradient(5)
     gradient(6)
-    assemble(3)
     gradient(7)
     gradient(8)
+    assemble(3)
     assemble(4)
-    assemble(5)
     gradient(9)
     early_gradient()
+    assemble(5)
     assemble(6)
     assemble(7)
     assemble(8)

time: 71.6 us -> 71.4 us (level)
  no operation moved by 1% of the time
where the time goes in v8:
time: 71.4 us; the launch traced here: 71.2 us
  Pallas kernels  70.5 us (99%)
    pallas_call x1, Pallas kernels, body(): pl.pallas_call(kernel, out_shape=(jax.ShapeDtypeStruct((2, sensors, funcs...  67.1 us
    pallas_call x1, Pallas kernels, body(): pl.pallas_call(weight_kernel, grid=(sensors // TILE,), out_shape=(jax.Sha...  3.4 us

profile of v8, /device:TPU:1, one launch (start us, length us, event | category | flops | bytes accessed | tf_op | source)
XLA Modules:
  0.0 71.2 jit_solution(15311329509831603477)
XLA Ops:
  0.6 67.1 %shard_map.67 = (bf16[2,2048,128]{2,1,0:T(8,128)(2,1)}, bf16[2048,512]{1,0:T(8,128)(2,1)}, bf16[256,512]{1,0:T(8,128)(2,1)}, f32[4,512]{1,0:T(4,128)}, f32[1,512]{1,0:T(1,128)}) custom-call(bf16[128,2048]{1,0:T(8,128)(2,1)} %samples.1, bf16[2048,512]{1,0:T(8,128)(2,1)} %weight.1, f32[512]{0:T(512)} %bias.1, bf16[4,512]{1,0:T(4,128)(2,1)} %upstream.1), custom_call_target="tpu_custom_call" | custom-call | tf_op jit(solution)/shard_map/pallas_call | solution.py:378
  67.8 3.4 %shard_map.68 = (bf16[2048,512]{1,0:T(8,128)(2,1)}, bf16[4,512]{1,0:T(4,128)(2,1)}, f32[512]{0:T(512)}) custom-call(bf16[2,2048,128]{2,1,0:T(8,128)(2,1)} %get-tuple-element.11.st, bf16[2048,512]{1,0:T(8,128)(2,1)} %get-tuple-element.12.early, bf16[256,512]{1,0:T(8,128)(2,1)} %get-tuple-element.13.g, f32[4,512]{1,0:T(4,128)} %get-tuple-element.14.act, ...), custom_call_target="tpu_custom_call" | custom-call | tf_op jit(solution)/shard_map/pallas_call | solution.py:415
